TPU v7x, 256 devices: a whole 4x4x8 slice. The times are simulated.
256 devices in a mesh: dp: 4 (over x), expert: 64 (over y, z, core).
Axes of the slice: x: 4, y: 4, z: 8, core: 2. Of those that a mesh axis runs over, the one named last changes fastest.
Arguments:
- tokens: bfloat16 [32768, 2048], P(('dp', 'expert')), may hold values from -6 to 6
- routes: int32 [32768, 8], P(('dp', 'expert')), may hold values from 0 to 127, all different within a row
- route_weight: float32 [32768, 8], P(('dp', 'expert')), may hold values from 0.05 to 0.5
- bias: float32 [128], replicated, may hold values from -3 to 3
- w_gate: bfloat16 [128, 768, 2048], P('expert', 'dp'), may hold values from -0.125 to 0.125
- w_up: bfloat16 [128, 768, 2048], P('expert', 'dp'), may hold values from -0.125 to 0.125
- w_down: bfloat16 [128, 768, 2048], P('expert', 'dp'), may hold values from -0.21875 to 0.21875
Outputs:
- mixed: bfloat16 [32768, 2048], P(('dp', 'expert'))
- new_bias: float32 [128], replicated
- counts: int32 [128], replicated
Inputs may be any that keep to these rules, and one draw needn't show every extreme that they name: `routes`: each token names 8 different experts.
All inputs are finite; a program needn't handle non-finite values.
Results may differ from a plain program's by a relative error of at most 0.0057.
Values may be sent and summed in bfloat16 or wider, within the bound.
A program may use at most 128 MiB of HBM per device.

v0:
```python
import jax
import jax.numpy as jnp
from jax import lax
from jax.sharding import Mesh
from jax.sharding import PartitionSpec as P

EXPERT = ("expert_0", "expert_1", "expert_2")
DP_EXPERT = ("dp", "expert_0", "expert_1", "expert_2")


bias_rate = 0.05


def sent_together(arrays, axis, dim, along):
    both = jnp.concatenate(arrays, axis=along)
    whole, at, outs = (lax.all_gather(both, axis, axis=dim, tiled=True), 0, [])
    for a in arrays:
        outs.append(lax.slice_in_dim(whole, at, at + a.shape[along], axis=along))
        at += a.shape[along]
    return tuple(outs)


def grouped_exchange(array, axis, split_dim, concat_dim, work, item_dim, out_dim):
    items = jax.tree.leaves(array)[0].shape[item_dim]
    count = 2 if items % 2 == 0 else 1
    outs = []
    for k in range(count):
        group = jax.tree.map(
            lambda a: lax.slice_in_dim(
                a, k * (items // count), (k + 1) * (items // count), axis=item_dim
            ),
            array,
        )
        outs.append(
            work(
                lax.all_to_all(
                    group, axis, split_axis=split_dim, concat_axis=concat_dim, tiled=True
                )
            )
        )
    return jax.tree.map(lambda *parts: jnp.concatenate(parts, axis=out_dim), *outs)


def over_axes(array, axes):
    for axis in axes:
        array = lax.psum(array, axis)
    return array


def expert_products(received, gate_w, up_w, down_w):
    gate_act = jnp.einsum("sjcd,jfd->sjcf", received, gate_w, preferred_element_type=jnp.float32)
    up_act = jnp.einsum("sjcd,jfd->sjcf", received, up_w, preferred_element_type=jnp.float32)
    hidden = (jax.nn.silu(gate_act) * up_act).astype(jnp.bfloat16)
    return jnp.einsum("sjcf,jfd->sjcd", hidden, down_w, preferred_element_type=jnp.float32)


def body(tokens, routes, route_weight, bias, w_gate, w_up, w_down):
    tok_rows, feature_width = tokens.shape
    top_count = routes.shape[1]
    experts = bias.shape[0]
    groups = lax.axis_size(EXPERT)
    per_device = w_gate.shape[0]
    capacity = 5 * tok_rows * top_count // (4 * experts)
    flat_routes = routes.reshape(-1)
    labels = jnp.arange(experts, dtype=jnp.int32)
    picked = (flat_routes[:, None] == labels[None, :]).astype(jnp.int32)
    running = jnp.cumsum(picked, axis=0) - picked
    slot_rank = jnp.sum(running * picked, axis=1)
    local_counts = jnp.sum(picked, axis=0)
    kept_mask = slot_rank < capacity
    slot_total = experts * capacity
    slot_index = jnp.where(kept_mask, flat_routes * capacity + slot_rank, slot_total)
    token_index = jnp.arange(tok_rows * top_count, dtype=jnp.int32) // top_count
    source = jnp.zeros((slot_total + 1,), jnp.int32).at[slot_index].set(token_index)[:slot_total]
    filled = jnp.zeros((slot_total + 1,), jnp.bool_).at[slot_index].set(True)[:slot_total]
    send_rows = jnp.where(filled[:, None], tokens[source], jnp.zeros((), jnp.bfloat16))
    send_rows = send_rows.reshape(groups, per_device, capacity, feature_width)
    gathered = sent_together((w_gate, w_up, w_down), "dp", 1, 0)

    def serve_rows(received):
        produced = expert_products(received, gathered[0], gathered[1], gathered[2]).astype(
            jnp.bfloat16
        )
        return lax.all_to_all(produced, EXPERT, split_axis=0, concat_axis=0, tiled=True)

    returned = grouped_exchange(send_rows, EXPERT, 0, 0, serve_rows, 2, 2)
    flat_out = returned.reshape(slot_total, feature_width)
    fetched = flat_out[jnp.minimum(slot_index, slot_total - 1)]
    entry_weight = jnp.where(kept_mask, route_weight.reshape(-1), jnp.float32(0.0))
    weighted = fetched.astype(jnp.float32) * entry_weight[:, None]
    mixed = jnp.sum(weighted.reshape(tok_rows, top_count, feature_width), axis=1).astype(
        jnp.bfloat16
    )
    counts_float = local_counts.astype(jnp.float32)
    mean_load = tok_rows * top_count * lax.axis_size("dp") * groups
    totals = over_axes(counts_float, DP_EXPERT)
    new_bias = bias + bias_rate * jnp.sign(mean_load - experts * totals)
    return (mixed, new_bias, totals.astype(jnp.int32))


def solution(mesh):
    torus = Mesh(
        mesh.devices.reshape(mesh.shape["dp"], 4, 8, 2), ("dp", "expert_0", "expert_1", "expert_2")
    )
    placed = (
        P(DP_EXPERT, None),
        P(DP_EXPERT, None),
        P(DP_EXPERT, None),
        P(),
        P(EXPERT, "dp", None),
        P(EXPERT, "dp", None),
        P(EXPERT, "dp", None),
    )
    return jax.shard_map(
        body, mesh=torus, in_specs=placed, out_specs=(P(DP_EXPERT, None), P(), P()), check_vma=False
    )
```

profile of v0, /device:TPU:8, one launch (start us, length us, event | category | flops | bytes accessed | tf_op | source)
XLA Modules:
  0.0 419.1 jit_solution(14399067716921615982)
XLA Ops:
  7.2 4.1 pad_maximum_fusion.1
  13.5 4.3 %scatter_custom_fusion.1 = s32[1281]{0:T(1024)S(1)} fusion(s32[1024]{0:T(1024)S(1)} %bitcast.86, s32[1024]{0:T(1024)S(1)} %add_select_fusion, s32[]{:T(128)} %constant.15.clone.1), kind=kCustom, calls=%fused_computation.63 | custom fusion | bytes 5128 | tf_op jit(solution)/shard_map/scatter | solution.py:74
  17.8 6.2 %gather_fusion = bf16[1280,2048]{1,0:T(8,128)(2,1)} fusion(bf16[128,2048]{1,0:T(8,128)(2,1)S(1)} %copy-done, s32[2048]{0:T(1024)S(1)} %pad_clamp_fusion), kind=kCustom, calls=%fused_computation | custom fusion | bytes 10490880 | tf_op jit(solution)/shard_map/gather | solution.py:76
  24.0 9.9 %gather.9 = bf16[64,2,10,2048]{3,2,1,0:T(8,128)(2,1)} reshape(bf16[1280,2048]{1,0:T(8,128)(2,1)} %gather_fusion) | data formatting | bytes 10485760 | tf_op jit(solution)/shard_map/gather | solution.py:76
  33.9 4.8 %scatter_custom_fusion = pred[1281]{0:T(1024)(128)(4,1)S(1)} fusion(s32[1024]{0:T(1024)S(1)} %bitcast.87, pred[1024]{0:T(1024)(128)(4,1)S(1)} %broadcast.131, pred[]{:T(512)} %constant.18.clone.1), kind=kCustom, calls=%fused_computation.66 | custom fusion | bytes 1282 | tf_op jit(solution)/shard_map/scatter | solution.py:75
  38.9 7.7 %broadcast_select_fusion = bf16[64,2,10,2048]{3,2,1,0:T(8,128)(2,1)} fusion(bf16[64,2,10,2048]{3,2,1,0:T(8,128)(2,1)} %gather.9, pred[64,2,10]{2,1,0:T(4,128)(4,1)S(1)} %broadcast_in_dim.43), kind=kLoop, calls=%fused_computation.6 | loop fusion | flops 2621440 | bytes 10487040 | tf_op jit(solution)/shard_map/jit(_where)/select_n | solution.py:76
  46.6 7.2 %fusion.39 = (bf16[64,2,5,2048]{3,2,1,0:T(8,128)(2,1)S(1)}, bf16[64,2,5,2048]{3,2,1,0:T(8,128)(2,1)}) fusion(bf16[64,2,10,2048]{3,2,1,0:T(8,128)(2,1)} %broadcast_select_fusion), kind=kLoop, calls=%fused_computation.72 | loop fusion | bytes 10485760 | tf_op jit(solution)/shard_map/slice | solution.py:29
  53.8 4.7 %copy.37 = bf16[64,2,5,2048]{3,1,2,0:T(2,128)(2,1)} copy(bf16[64,2,5,2048]{3,2,1,0:T(8,128)(2,1)S(1)} %get-tuple-element.7) | data formatting | bytes 5242880 | tf_op jit(solution)/shard_map/slice | solution.py:29
  58.5 11.9 %all-to-all-start = ((bf16[64,2,5,2048]{3,1,2,0:T(2,128)(2,1)}), bf16[64,2,5,2048]{3,1,2,0:T(2,128)(2,1)S(1)}, u32[]{:S(2)}, u32[]{:S(2)}) async-start(bf16[64,2,5,2048]{3,1,2,0:T(2,128)(2,1)} %copy.37), calls=%async_computation | async-start | bytes 5242880 | tf_op jit(solution)/shard_map/all_to_all | solution.py:36
  70.4 6.8 %copy.41 = bf16[64,2,5,2048]{3,1,2,0:T(2,128)(2,1)} copy(bf16[64,2,5,2048]{3,2,1,0:T(8,128)(2,1)} %get-tuple-element.8) | data formatting | bytes 5242880 | tf_op jit(solution)/shard_map/slice | solution.py:29
  77.2 53.8 %all-to-all-done = bf16[64,2,5,2048]{3,1,2,0:T(2,128)(2,1)S(1)} async-done(((bf16[64,2,5,2048]{3,1,2,0:T(2,128)(2,1)}), bf16[64,2,5,2048]{3,1,2,0:T(2,128)(2,1)S(1)}, u32[]{:S(2)}, u32[]{:S(2)}) %all-to-all-start) | async-done | bytes 2621472 | tf_op jit(solution)/shard_map/all_to_all | solution.py:36
  132.5 7.6 %all-to-all-start.2 = ((bf16[64,2,5,2048]{3,1,2,0:T(2,128)(2,1)}), bf16[64,2,5,2048]{3,1,2,0:T(2,128)(2,1)S(1)}, u32[]{:S(2)}, u32[]{:S(2)}) async-start(bf16[64,2,5,2048]{3,1,2,0:T(2,128)(2,1)} %copy.41), calls=%async_computation.2 | async-start | bytes 5242880 | tf_op jit(solution)/shard_map/all_to_all | solution.py:36
  140.1 48.9 %all-gather.2.cloned.1.call-done = bf16[6,768,2048]{2,1,0:T(8,128)(2,1)} async-done(((bf16[6,192,2048]{2,1,0:T(8,128)(2,1)}), bf16[6,768,2048]{2,1,0:T(8,128)(2,1)}) %all-gather.2.cloned.1.call-update) | async-done | bytes 18874384 | tf_op jit(solution)/shard_map/all_gather | solution.py:16
  189.0 6.7 %fusion.4 = f32[2,768,64,5]{1,2,3,0:T(8,128)S(1)} fusion(bf16[6,768,2048]{2,1,0:T(8,128)(2,1)} %all-gather.2.cloned.1.call-done, bf16[64,2,5,2048]{3,1,2,0:T(2,128)(2,1)} %copy-done.4), kind=kOutput, calls=%fused_computation.14 | convolution fusion | flops 2013265920 | bytes 10878976 | tf_op jit(solution)/shard_map/sjcd,jfd->sjcf/dot_general | solution.py:51
  195.7 5.9 %fusion.19 = bf16[64,2,5,768]{3,0,2,1:T(8,128)(2,1)S(1)} fusion(f32[2,768,64,5]{1,2,3,0:T(8,128)S(1)} %fusion.4, bf16[64,2,5,2048]{3,1,2,0:T(2,128)(2,1)S(1)} %copy-done.5, bf16[6,768,2048]{2,1,0:T(8,128)(2,1)} %all-gather.2.cloned.1.call-done), kind=kOutput, calls=%fused_computation.34 | convolution fusion | flops 2016215040 | bytes 11862016 | tf_op jit(solution)/shard_map/sjcd,jfd->sjcf/dot_general | solution.py:52
  201.7 5.0 %fusion.10 = bf16[64,2,5,2048]{3,0,2,1:T(8,128)(2,1)S(1)} fusion(bf16[64,2,5,768]{3,0,2,1:T(8,128)(2,1)S(1)} %fusion.19, bf16[6,768,2048]{2,1,0:T(8,128)(2,1)} %all-gather.2.cloned.1.call-done), kind=kOutput, calls=%fused_computation.21 | convolution fusion | flops 2014576640 | bytes 9895936 | tf_op jit(solution)/shard_map/sjcf,jfd->sjcd/dot_general | solution.py:54
  206.7 4.2 %copy.40 = bf16[64,2,5,2048]{3,1,2,0:T(2,128)(2,1)} copy(bf16[64,2,5,2048]{3,0,2,1:T(8,128)(2,1)S(1)} %fusion.10) | data formatting | bytes 5242880 | tf_op jit(solution)/shard_map/convert_element_type | solution.py:81
  212.4 10.6 %all-to-all-start.1 = ((bf16[64,2,5,2048]{3,1,2,0:T(2,128)(2,1)}), bf16[64,2,5,2048]{3,1,2,0:T(2,128)(2,1)S(1)}, u32[]{:S(2)}, u32[]{:S(2)}) async-start(bf16[64,2,5,2048]{3,1,2,0:T(2,128)(2,1)} %copy.40), calls=%async_computation.1 | async-start | bytes 5242880 | tf_op jit(solution)/shard_map/all_to_all | solution.py:84
  222.9 6.7 %fusion.3 = f32[2,768,64,5]{1,2,3,0:T(8,128)S(1)} fusion(bf16[6,768,2048]{2,1,0:T(8,128)(2,1)} %all-gather.2.cloned.1.call-done, bf16[64,2,5,2048]{3,1,2,0:T(2,128)(2,1)} %copy-done.2), kind=kOutput, calls=%fused_computation.13 | convolution fusion | flops 2013265920 | bytes 10878976 | tf_op jit(solution)/shard_map/sjcd,jfd->sjcf/dot_general | solution.py:51
  229.6 5.9 %fusion.15 = bf16[64,2,5,768]{3,0,2,1:T(8,128)(2,1)S(1)} fusion(f32[2,768,64,5]{1,2,3,0:T(8,128)S(1)} %fusion.3, bf16[64,2,5,2048]{3,1,2,0:T(2,128)(2,1)S(1)} %copy-done.3, bf16[6,768,2048]{2,1,0:T(8,128)(2,1)} %all-gather.2.cloned.1.call-done), kind=kOutput, calls=%fused_computation.27 | convolution fusion | flops 2016215040 | bytes 11862016 | tf_op jit(solution)/shard_map/sjcd,jfd->sjcf/dot_general | solution.py:52
  235.5 5.0 %fusion.9 = bf16[64,2,5,2048]{3,0,2,1:T(8,128)(2,1)S(1)} fusion(bf16[64,2,5,768]{3,0,2,1:T(8,128)(2,1)S(1)} %fusion.15, bf16[6,768,2048]{2,1,0:T(8,128)(2,1)} %all-gather.2.cloned.1.call-done), kind=kOutput, calls=%fused_computation.20 | convolution fusion | flops 2014576640 | bytes 9895936 | tf_op jit(solution)/shard_map/sjcf,jfd->sjcd/dot_general | solution.py:54
  240.6 4.2 %copy.44 = bf16[64,2,5,2048]{3,1,2,0:T(2,128)(2,1)} copy(bf16[64,2,5,2048]{3,0,2,1:T(8,128)(2,1)S(1)} %fusion.9) | data formatting | bytes 5242880 | tf_op jit(solution)/shard_map/convert_element_type | solution.py:81
  244.8 38.8 %all-to-all-done.1 = bf16[64,2,5,2048]{3,1,2,0:T(2,128)(2,1)S(1)} async-done(((bf16[64,2,5,2048]{3,1,2,0:T(2,128)(2,1)}), bf16[64,2,5,2048]{3,1,2,0:T(2,128)(2,1)S(1)}, u32[]{:S(2)}, u32[]{:S(2)}) %all-to-all-start.1) | async-done | bytes 2621472 | tf_op jit(solution)/shard_map/all_to_all | solution.py:84
  283.5 7.5 %all-to-all-start.3 = ((bf16[64,2,5,2048]{3,1,2,0:T(2,128)(2,1)}), bf16[64,2,5,2048]{3,1,2,0:T(2,128)(2,1)}, u32[]{:S(2)}, u32[]{:S(2)}) async-start(bf16[64,2,5,2048]{3,1,2,0:T(2,128)(2,1)} %copy.44), calls=%async_computation.3 | async-start | bytes 5242880 | tf_op jit(solution)/shard_map/all_to_all | solution.py:84
  291.3 8.7 %psum.28 = f32[128]{0:T(128)S(1)} all-reduce(f32[128]{0:T(128)S(1)} %convert_element_type.52), channel_id=1, replica_groups=mesh['dp'=4,'expert_0'=4,'expert_1'=8,'expert_2'=2] {'dp'}, use_global_device_ids=true, to_apply=%region_7.8 | all-reduce | flops 128 | bytes 1024 | tf_op jit(solution)/shard_map/psum | solution.py:46
  300.0 8.8 %psum.29 = f32[128]{0:T(128)S(1)} all-reduce(f32[128]{0:T(128)S(1)} %psum.28), channel_id=1, replica_groups=mesh['dp'=4,'expert_0'=4,'expert_1'=8,'expert_2'=2] {'expert_0'}, use_global_device_ids=true, to_apply=%region_8.9 | all-reduce | flops 128 | bytes 1024 | tf_op jit(solution)/shard_map/psum | solution.py:46
  308.7 51.1 %psum.30 = f32[128]{0:T(128)S(1)} all-reduce(f32[128]{0:T(128)S(1)} %psum.29), channel_id=1, replica_groups=mesh['dp'=4,'expert_0'=4,'expert_1'=8,'expert_2'=2] {'expert_1'}, use_global_device_ids=true, to_apply=%region_9.10 | all-reduce | flops 128 | bytes 1024 | tf_op jit(solution)/shard_map/psum | solution.py:46
  362.9 13.3 %pad_maximum_fusion = bf16[64,2,10,2048]{3,1,2,0:T(2,128)(2,1)S(1)} fusion(bf16[64,2,5,2048]{3,1,2,0:T(2,128)(2,1)} %all-to-all-done.3, bf16[64,2,5,2048]{3,1,2,0:T(2,128)(2,1)S(1)} %all-to-all-done.1), kind=kLoop, calls=%fused_computation.10 | loop fusion | flops 2621440 | bytes 10485760 | tf_op jit(solution)/shard_map/concatenate | solution.py:41
  376.2 6.4 %copy.45 = bf16[64,2,10,2048]{3,2,1,0:T(8,128)(2,1)} copy(bf16[64,2,10,2048]{3,1,2,0:T(2,128)(2,1)S(1)} %pad_maximum_fusion) | data formatting | bytes 10485760 | tf_op jit(solution)/shard_map/concatenate | solution.py:41
  382.6 9.8 %reshape.109 = bf16[1280,2048]{1,0:T(8,128)(2,1)} reshape(bf16[64,2,10,2048]{3,2,1,0:T(8,128)(2,1)} %copy.45) | data formatting | bytes 10485760 | tf_op jit(solution)/shard_map/reshape | solution.py:87
  392.4 12.0 %gather_fusion.1 = bf16[1024,2048]{1,0:T(8,128)(2,1)} fusion(bf16[1280,2048]{1,0:T(8,128)(2,1)} %reshape.109, s32[1024]{0:T(1024)S(1)} %broadcast_clamp_fusion), kind=kCustom, calls=%fused_computation.1 | custom fusion | bytes 8392704 | tf_op jit(solution)/shard_map/gather | solution.py:88
  404.5 7.3 %fusion = bf16[128,2048]{1,0:T(8,128)(2,1)} fusion(bf16[1024,2048]{1,0:T(8,128)(2,1)} %gather_fusion.1, f32[128,8]{1,0:T(8,128)S(1)} %broadcast_select_fusion.1), kind=kLoop, calls=%fused_computation.5 | loop fusion | flops 6029312 | bytes 4722688 | tf_op jit(solution)/shard_map/reduce_sum | solution.py:91
  (51 shorter events, 8.5 us)
Async XLA Ops:
  7.2 10.6 %copy-start = (bf16[128,2048]{1,0:T(8,128)(2,1)S(1)}, bf16[128,2048]{1,0:T(8,128)(2,1)}, u32[]{:S(2)}) copy-start(bf16[128,2048]{1,0:T(8,128)(2,1)} %param.7) | copy-start | bytes 1572868
  7.2 181.9 %all-gather.2.cloned.1.call-start = ((), (), s32[]{:S(2)}) async-start(), calls=%async_computation.4 | async-start | bytes 23592960 | tf_op jit(solution)/shard_map/all_gather | solution.py:16
  11.4 0.7 copy-start.6
  58.5 72.5 %all-to-all-start = ((bf16[64,2,5,2048]{3,1,2,0:T(2,128)(2,1)}), bf16[64,2,5,2048]{3,1,2,0:T(2,128)(2,1)S(1)}, u32[]{:S(2)}, u32[]{:S(2)}) async-start(bf16[64,2,5,2048]{3,1,2,0:T(2,128)(2,1)} %copy.37), calls=%async_computation | async-start | bytes 5242880 | tf_op jit(solution)/shard_map/all_to_all | solution.py:36
  131.0 1.5 copy-start.4
  132.5 78.4 %all-to-all-start.2 = ((bf16[64,2,5,2048]{3,1,2,0:T(2,128)(2,1)}), bf16[64,2,5,2048]{3,1,2,0:T(2,128)(2,1)S(1)}, u32[]{:S(2)}, u32[]{:S(2)}) async-start(bf16[64,2,5,2048]{3,1,2,0:T(2,128)(2,1)} %copy.41), calls=%async_computation.2 | async-start | bytes 5242880 | tf_op jit(solution)/shard_map/all_to_all | solution.py:36
  189.0 6.7 %copy-start.5 = (bf16[64,2,5,2048]{3,1,2,0:T(2,128)(2,1)S(1)}, bf16[64,2,5,2048]{3,1,2,0:T(2,128)(2,1)}, u32[]{:S(2)}) copy-start(bf16[64,2,5,2048]{3,1,2,0:T(2,128)(2,1)} %copy-done.4) | copy-start | bytes 7864324
  210.9 1.5 copy-start.2
  212.4 71.2 %all-to-all-start.1 = ((bf16[64,2,5,2048]{3,1,2,0:T(2,128)(2,1)}), bf16[64,2,5,2048]{3,1,2,0:T(2,128)(2,1)S(1)}, u32[]{:S(2)}, u32[]{:S(2)}) async-start(bf16[64,2,5,2048]{3,1,2,0:T(2,128)(2,1)} %copy.40), calls=%async_computation.1 | async-start | bytes 5242880 | tf_op jit(solution)/shard_map/all_to_all | solution.py:84
  222.9 6.7 %copy-start.3 = (bf16[64,2,5,2048]{3,1,2,0:T(2,128)(2,1)S(1)}, bf16[64,2,5,2048]{3,1,2,0:T(2,128)(2,1)}, u32[]{:S(2)}) copy-start(bf16[64,2,5,2048]{3,1,2,0:T(2,128)(2,1)} %copy-done.2) | copy-start | bytes 7864324
  240.6 50.6 %copy-start.7 = (f32[128,8]{0,1:T(8,128)S(1)}, f32[128,8]{0,1:T(8,128)}, u32[]{:S(2)}) copy-start(f32[128,8]{0,1:T(8,128)} %param.9) | copy-start | bytes 12292
  240.6 121.8 %copy-start.8 = (f32[128]{0:T(128)S(1)}, f32[128]{0:T(128)}, u32[]{:S(2)}) copy-start(f32[128]{0:T(128)} %param.10) | copy-start | bytes 1540
  283.5 79.3 %all-to-all-start.3 = ((bf16[64,2,5,2048]{3,1,2,0:T(2,128)(2,1)}), bf16[64,2,5,2048]{3,1,2,0:T(2,128)(2,1)}, u32[]{:S(2)}, u32[]{:S(2)}) async-start(bf16[64,2,5,2048]{3,1,2,0:T(2,128)(2,1)} %copy.44), calls=%async_computation.3 | async-start | bytes 5242880 | tf_op jit(solution)/shard_map/all_to_all | solution.py:84
  392.4 19.4 %copy-start.1 = (bf16[128,2048]{1,0:T(8,128)(2,1)S(1)}, bf16[128,2048]{1,0:T(8,128)(2,1)}, u32[]{:S(2)}) copy-start(bf16[128,2048]{1,0:T(8,128)(2,1)} %param.7) | copy-start | bytes 1572868
Sparse Core Ops, SparseCore 0:
  11.5 177.4 all-gather.1
where the time goes:
time: 427 us; the launch traced here: 419 us
  waiting for transfers between devices  141 us (33%)
  local copies, waits for them, and re-layouts  85.4 us (20%)
  blocking collectives  71 us (17%)
  starting transfers between devices  37.6 us (9%)
  matrix products  35.2 us (8%)
  other arithmetic  33.6 us (8%)
  between operations  14.8 us (3%)
    psum x4, blocking collectives, over_axes(): array = lax.psum(array, axis)  71 us
    all_to_all x2, waiting for transfers between devices, grouped_exchange(): lax.all_to_all(group, axis, split_axis=split_dim, concat_axis=concat_dim,...  53.8 us
    all_gather x1, waiting for transfers between devices, sent_together(): whole, at, outs = (lax.all_gather(both, axis, axis=dim, tiled=True), 0, [])  48.9 us
    all_to_all x2, waiting for transfers between devices, serve_rows(): lax.all_to_all(produced, EXPERT, split_axis=0, concat_axis=0, tiled=True)  38.8 us
    all_to_all x2, starting transfers between devices, grouped_exchange(): lax.all_to_all(group, axis, split_axis=split_dim, concat_axis=concat_dim,...  19.5 us
    slice x3, local copies, waits for them, and re-layouts, grouped_exchange(): lax.slice_in_dim(a, k * (items // count), (k + 1) * (items // count), axi...  18.8 us
    all_to_all x2, starting transfers between devices, serve_rows(): lax.all_to_all(produced, EXPERT, split_axis=0, concat_axis=0, tiled=True)  18.1 us
    gather x2, local copies, waits for them, and re-layouts, body(): tokens[source]  16 us
  transfers between devices with their start and end apart: 5, of which 3 were waited for; matrix products, arithmetic and copies ran while one was open for 23% of the time, Pallas kernels for 0%

commit v1 on v0

v1 whole, which is shorter than its diff:
```python
import functools

import jax
import jax.numpy as jnp
from jax import lax
from jax.experimental import pallas as pl
from jax.experimental.pallas import tpu as pltpu
from jax.sharding import Mesh
from jax.sharding import PartitionSpec as P

EXPERT = ("expert_0", "expert_1", "expert_2")
DP_EXPERT = ("dp", "expert_0", "expert_1", "expert_2")
MESH = pl.DeviceIdType.MESH
BF16, F32 = jnp.bfloat16, jnp.float32

NX, NY, NZ, NCORE = 4, 4, 8, 2
PER = 2
CAP = 10
NS = NY * NCORE
SLOTS = CAP * NZ
NC = 8
bias_rate = 0.05

NT = (((1,), (1,)), ((), ()))


def wrap(v, n):
    return lax.rem(v + 2 * n, n)


def kernel(
    meta_ref, bias_ref, tok_ref, wg_ref, wu_ref, wd_ref,
    out_ref, cnt_ref, nb_ref,
    xb, pm, wh, wl, sb, rb, cb, wgu, wdn, hid, rl1, rl2, rsb, meta, keys, wks, csend, crecv,
    loc_s, tok_s, wdl_s, meta_ss, meta_rs, c_ss, c_rs,
    z_ss, z_rs, y1_ss, y1_rs, l1_rs, f1_ss, y2_ss, y2_rs, l2_rs, f2_ss, r_ss, r_rs,
    g_ss, g_rs, d_ss, d_rs,
):
    x, y = lax.axis_index("dp"), lax.axis_index("expert_0")
    z, c = lax.axis_index("expert_1"), lax.axis_index("expert_2")
    feat = tok_ref.shape[1]
    width = feat // NC
    tok = tok_ref.shape[0]
    ff = wg_ref.shape[1]
    xp, xm = wrap(x + 1, NX), wrap(x - 1, NX)
    yp, ym = wrap(y + 1, NY), wrap(y - 1, NY)
    other = 1 - c
    mine = y * NCORE + c
    home = (x, y, z, c)

    def rcopy(src, dst, ss, rs, to):
        return pltpu.make_async_remote_copy(
            src_ref=src, dst_ref=dst, send_sem=ss, recv_sem=rs, device_id=to, device_id_type=MESH
        )

    def got(ref, sem):
        rcopy(ref, ref, sem, sem, (xp, y, z, c)).wait_recv()

    def sent(ref, sem):
        rcopy(ref, ref, sem, sem, (xp, y, z, c)).wait_send()

    own_g = [
        pltpu.make_async_copy(wg_ref, wgu.at[0, :, x], loc_s.at[0]),
        pltpu.make_async_copy(wu_ref, wgu.at[1, :, x], loc_s.at[1]),
    ]
    own_g[0].start()
    own_g[1].start()

    def columns(k):
        return pl.ds(pl.multiple_of(k * width, width), width)

    def tok_copy(k):
        return pltpu.make_async_copy(tok_ref.at[:, columns(k)], xb.at[k, z], tok_s.at[k])

    def wd_copy(k):
        return pltpu.make_async_copy(wd_ref.at[:, :, columns(k)], wdn.at[k, :, x], wdl_s.at[k])

    @pl.loop(0, NC)
    def _(k):
        tok_copy(k).start()

    @pl.loop(0, NC)
    def _(k):
        wd_copy(k).start()

    barrier = pltpu.get_barrier_semaphore()
    peers = [(xp, y, z, c), (xm, y, z, c), (x, y, z, other)]
    peers += [(x, yy, z, cc) for yy in (yp, ym) for cc in range(NCORE)]
    peers += [(x, y, wrap(z + o, NZ), c) for o in range(1, NZ)]
    for p in peers:
        pl.semaphore_signal(barrier, inc=1, device_id=p, device_id_type=MESH)
    pl.semaphore_wait(barrier, len(peers))

    for o in range(1, NZ):
        rcopy(meta_ref, meta.at[z], meta_ss, meta_rs, (x, y, wrap(z + o, NZ), c)).start()
    meta[z] = meta_ref[...]

    def z_hop(k, h):
        s = 1 - 2 * lax.rem(k, 2)
        far = wrap(z - s * (h - 1), NZ)
        near = wrap(z + s * (h - 1), NZ)
        if h >= 2:
            got(xb.at[k, far], z_rs.at[k, 0, h - 2])
        rcopy(
            xb.at[k, far], xb.at[k, far], z_ss.at[k], z_rs.at[k, 0, h - 1],
            (x, y, wrap(z + s, NZ), c),
        ).start()
        if h >= 4:
            return
        if h >= 2:
            got(xb.at[k, near], z_rs.at[k, 1, h - 2])
        rcopy(
            xb.at[k, near], xb.at[k, near], z_ss.at[k], z_rs.at[k, 1, h - 1],
            (x, y, wrap(z - s, NZ), c),
        ).start()

    def z_own(k):
        tok_copy(k).wait()
        z_hop(k, 1)

    z_own(0)
    z_own(1)

    own_g[0].wait()
    own_g[1].wait()

    def g_piece(w, j, xs):
        return wgu.at[w, j, xs]

    for j in range(PER):
        for w in range(2):
            a, b = g_piece(w, j, x), g_piece(w, 1 - j, x)
            rcopy(a, a, g_ss.at[0, w * PER + j], g_rs.at[0, w * PER + j], (xp, y, z, c)).start()
            i = w * PER + 1 - j
            rcopy(b, b, g_ss.at[1, i], g_rs.at[1, i], (xm, y, z, c)).start()

    def g_relay(w):
        got(g_piece(w, 0, xm), g_rs.at[0, w * PER])
        a = g_piece(w, 0, xm)
        rcopy(a, a, g_ss.at[2, w], g_rs.at[2, w], (xp, y, z, c)).start()
        got(g_piece(w, 1, xp), g_rs.at[1, w * PER + 1])
        b = g_piece(w, 1, xp)
        rcopy(b, b, g_ss.at[3, w], g_rs.at[3, w], (xm, y, z, c)).start()

    got(meta.at[pl.ds(0, NZ - 1)], meta_rs)
    row = lax.broadcasted_iota(jnp.int32, (NS * PER, tok), 0)
    expert = ((row // 4) * (NZ * 4) + z * 4 + row % 4).astype(F32)
    before = (
        lax.broadcasted_iota(jnp.int32, (tok, tok), 0)
        < lax.broadcasted_iota(jnp.int32, (tok, tok), 1)
    ).astype(F32).astype(BF16)
    slot_row = lax.broadcasted_iota(jnp.int32, (NS * PER, SLOTS, tok), 1).astype(F32)

    @pl.loop(0, NZ)
    def _(b):
        hit = jnp.zeros((NS * PER, tok), F32)
        weight = jnp.zeros((NS * PER, tok), F32)
        for k in range(8):
            same = meta[b, k : k + 1, :] == expert
            hit = jnp.where(same, 1.0, hit)
            weight = jnp.where(same, meta[b, 8 + k : 9 + k, :], weight)
        rank = jnp.dot(hit.astype(BF16), before, preferred_element_type=F32)
        key = jnp.where(hit > 0.0, rank * NZ + b.astype(F32), -1.0)
        keys[b] = key
        wks[b] = weight
        pick = jnp.where(key[:, None, :] == slot_row, 1.0, 0.0)
        at = pl.ds(pl.multiple_of(b * tok, tok), tok)
        pm[:, at] = pick.reshape(NS * PER * SLOTS, tok).astype(BF16)

    def y_send(k, src, dst, rl, ss, rs, ls):
        rcopy(src.at[k, y * NCORE + other], dst.at[k, mine], ss.at[k], rs.at[k], (x, y, z, other)).start()
        for cc, yf, to in ((0, yp, 0), (1, ym, 1)):
            opp = wrap(y + 2, NY)
            rcopy(src.at[k, opp * NCORE + cc], rl.at[k, to], ss.at[k], ls.at[k, to], (x, yf, z, c)).start()
        for yy in (yp, ym):
            for cc in range(NCORE):
                rcopy(src.at[k, yy * NCORE + cc], dst.at[k, mine], ss.at[k], rs.at[k], (x, yy, z, cc)).start()

    def y_forward(k, dst, rl, fs, rs, ls):
        got(rl.at[k, 0], ls.at[k, 0])
        rcopy(rl.at[k, 0], dst.at[k, ym * NCORE + c], fs.at[k], rs.at[k], (x, yp, z, 0)).start()
        got(rl.at[k, 1], ls.at[k, 1])
        rcopy(rl.at[k, 1], dst.at[k, yp * NCORE + c], fs.at[k], rs.at[k], (x, ym, z, 1)).start()

    def pick_rows(k):
        s = 1 - 2 * lax.rem(k, 2)
        got(xb.at[k, wrap(z + 4, NZ)], z_rs.at[k, 0, 3])
        got(xb.at[k, wrap(z + 3 * s, NZ)], z_rs.at[k, 1, 2])
        half = NS * PER * SLOTS // 2

        @pl.loop(0, 2)
        def _(p):
            rows = pm[pl.ds(pl.multiple_of(p * half, half), half), :]
            picked = jnp.dot(rows, xb[k].reshape(NZ * tok, width), preferred_element_type=F32)
            picked = picked.astype(BF16).reshape(NS // 2, PER, SLOTS, width)
            sb[k, pl.ds(p * (NS // 2), NS // 2)] = picked

        rb[k, mine] = sb[k, mine]
        y_send(k, sb, rb, rl1, y1_ss, y1_rs, l1_rs)

    def guarded(k, fn):
        @pl.when(jnp.logical_and(k >= 0, k < NC))
        def _():
            fn(k)

    @pl.loop(0, NC + 4)
    def _(i):
        guarded(i - 2, lambda k: z_hop(k, 4))
        guarded(i - 1, lambda k: z_hop(k, 3))
        guarded(i, lambda k: z_hop(k, 2))
        guarded(i + 2, z_own)
        guarded(i - 3, pick_rows)
        guarded(i - 4, lambda k: y_forward(k, rb, rl1, f1_ss, y1_rs, l1_rs))

        @pl.when(i == 5)
        def _():
            g_relay(0)

        @pl.when(i == 8)
        def _():
            g_relay(1)

    def d_own(k):
        wd_copy(k).wait()
        a = wdn.at[k, :, x]
        rcopy(a, a, d_ss.at[k, 0], d_rs.at[k, 0], (xp, y, z, c)).start()
        rcopy(a, a, d_ss.at[k, 1], d_rs.at[k, 1], (xm, y, z, c)).start()

    def d_relay(k):
        got(wdn.at[k, :, xm], d_rs.at[k, 0])
        a = wdn.at[k, 0, xm]
        rcopy(a, a, d_ss.at[k, 2], d_rs.at[k, 2], (xp, y, z, c)).start()
        got(wdn.at[k, :, xp], d_rs.at[k, 1])
        b = wdn.at[k, 1, xp]
        rcopy(b, b, d_ss.at[k, 3], d_rs.at[k, 3], (xm, y, z, c)).start()

    d_own(0)
    d_own(1)

    expert_row = lax.broadcasted_iota(jnp.int32, (tok, tok), 0).astype(F32)

    def count(b, total):
        hit = jnp.zeros((tok, tok), F32)
        for k in range(8):
            hit = jnp.where(meta[b, k : k + 1, :] == expert_row, 1.0, hit)
        ones = jnp.ones((8, tok), BF16)
        return total + lax.dot_general(ones, hit.astype(BF16), NT, preferred_element_type=F32)

    total = lax.fori_loop(0, NZ, count, jnp.zeros((8, tok), F32))
    y1 = y + 1 - 2 * lax.rem(y, 2)
    x1 = x + 1 - 2 * lax.rem(x, 2)
    partners = [(x, y, z, other), (x, y1, z, c), (x, NY - 1 - y, z, c), (x1, y, z, c), (NX - 1 - x, y, z, c)]
    csend[0] = total

    @pl.loop(0, NZ)
    def _(b):
        same = keys[b][:, None, :] == slot_row
        placed = jnp.where(same, wks[b][:, None, :], 0.0).reshape(NS * PER * SLOTS, tok).T
        high = placed.astype(BF16)
        wh[b] = high
        wl[b] = (placed - high.astype(F32)).astype(BF16)

    for s, to in enumerate(partners):
        move = rcopy(csend.at[s], crecv.at[s], c_ss.at[s], c_rs.at[s], to)
        move.start()
        move.wait()
        total = csend[s] + crecv[s]
        if s + 1 < len(partners):
            csend[s + 1] = total
    totals = total[0:1]
    cnt_ref[...] = totals.astype(jnp.int32)
    over = float(tok * 8 * NX * NY * NZ * NCORE) - float(tok) * totals
    sign = jnp.where(over > 0.0, 1.0, jnp.where(over < 0.0, -1.0, 0.0))
    nb_ref[...] = bias_ref[...] + bias_rate * sign

    @pl.loop(0, NC)
    def _(k):
        got(rb.at[k, pl.ds(0, NS - 1)], y1_rs.at[k])
        sent(xb.at[k, pl.ds(0, NZ - 1)], z_ss.at[k])
        sent(sb.at[k, pl.ds(0, NS - 1)], y1_ss.at[k])
        sent(rl1.at[k], f1_ss.at[k])

    sent(meta.at[pl.ds(0, NZ - 1)], meta_ss)

    def hidden_of(xs):
        @pl.loop(0, 2 * PER)
        def _(t):
            j = t // 2
            part = pl.ds((t % 2) * (NS // 2), NS // 2)
            gate = up = None
            for k in range(NC):
                rows = rb[k, part, j].reshape(NS // 2 * SLOTS, width)
                cols = slice(k * width, (k + 1) * width)
                g = lax.dot_general(rows, wgu[0, j, xs, :, cols], NT, preferred_element_type=F32)
                u = lax.dot_general(rows, wgu[1, j, xs, :, cols], NT, preferred_element_type=F32)
                gate = g if gate is None else gate + g
                up = u if up is None else up + u
            act = (gate / (1.0 + jnp.exp(-gate)) * up).astype(BF16)
            half = NS // 2 * SLOTS
            hid[j, xs, pl.ds(pl.multiple_of((t % 2) * half, half), half), :] = act

    @pl.loop(0, NX)
    def _(step):
        off = step + (step // 2) * (1 - 2 * (step % 2))
        xs = wrap(x + off, NX)

        @pl.when(step == 1)
        def _():
            for i in (0, 2):
                got(g_piece(i // PER, i % PER, xp), g_rs.at[1, i])

        @pl.when(step == 2)
        def _():
            for i in (1, 3):
                got(g_piece(i // PER, i % PER, xm), g_rs.at[0, i])

        @pl.when(step == 3)
        def _():
            opp = wrap(x + 2, NX)
            for w in range(2):
                got(g_piece(w, 0, opp), g_rs.at[2, w])
                got(g_piece(w, 1, opp), g_rs.at[3, w])

        hidden_of(xs)

    def down(k):
        opp = wrap(x + 2, NX)
        got(wdn.at[k, 0, opp], d_rs.at[k, 2])
        got(wdn.at[k, 1, opp], d_rs.at[k, 3])

        @pl.loop(0, PER)
        def _(j):
            total = None
            for xs in range(NX):
                t = jnp.dot(hid[j, xs], wdn[k, j, xs], preferred_element_type=F32)
                total = t if total is None else total + t
            sb[k, :, j] = total.astype(BF16).reshape(NS, SLOTS, width)

        cb[k, mine] = sb[k, mine]
        y_send(k, sb, cb, rl2, y2_ss, y2_rs, l2_rs)

    def far_send(k, h):
        s = 1 - 2 * lax.rem(k, 2)
        t = wrap(z + (5 - h) * s, NZ)
        if h >= 2:
            got(rsb.at[k, 0, h - 2], r_rs.at[k, 0, h - 2])
            xb[k, t] = (xb[k, t].astype(F32) + rsb[k, 0, h - 2].astype(F32)).astype(BF16)
        rcopy(xb.at[k, t], rsb.at[k, 0, h - 1], r_ss.at[k], r_rs.at[k, 0, h - 1], (x, y, wrap(z + s, NZ), c)).start()

    def near_send(k, h):
        s = 1 - 2 * lax.rem(k, 2)
        t = wrap(z - (4 - h) * s, NZ)
        if h >= 2:
            got(rsb.at[k, 1, h - 2], r_rs.at[k, 1, h - 2])
            xb[k, t] = (xb[k, t].astype(F32) + rsb[k, 1, h - 2].astype(F32)).astype(BF16)
        rcopy(xb.at[k, t], rsb.at[k, 1, h - 1], r_ss.at[k], r_rs.at[k, 1, h - 1], (x, y, wrap(z - s, NZ), c)).start()

    def combine(k):
        got(cb.at[k, pl.ds(0, NS - 1)], y2_rs.at[k])

        @pl.loop(0, 2)
        def _(p):
            part = pl.ds(p * (NZ // 2), NZ // 2)
            served = cb[k].reshape(NS * PER * SLOTS, width)
            hi = wh[part].reshape(NZ // 2 * tok, NS * PER * SLOTS)
            lo = wl[part].reshape(NZ // 2 * tok, NS * PER * SLOTS)
            summed = jnp.dot(hi, served, preferred_element_type=F32)
            summed += jnp.dot(lo, served, preferred_element_type=F32)
            xb[k, part] = summed.astype(BF16).reshape(NZ // 2, tok, width)

        far_send(k, 1)
        near_send(k, 1)

    def both(k, h):
        far_send(k, h)
        near_send(k, h)

    def finish(k):
        got(rsb.at[k, 0, 3], r_rs.at[k, 0, 3])
        got(rsb.at[k, 1, 2], r_rs.at[k, 1, 2])
        value = xb[k, z].astype(F32) + rsb[k, 0, 3].astype(F32) + rsb[k, 1, 2].astype(F32)
        out_ref[:, columns(k)] = value.astype(BF16)

    def feed(k):
        d_relay(k)
        guarded(k + 2, d_own)

    @pl.loop(0, NC + 7)
    def _(i):
        guarded(i - 7, finish)
        guarded(i - 6, lambda k: far_send(k, 4))
        guarded(i - 5, lambda k: both(k, 3))
        guarded(i - 4, lambda k: both(k, 2))
        guarded(i - 3, combine)
        guarded(i - 2, lambda k: y_forward(k, cb, rl2, f2_ss, y2_rs, l2_rs))
        guarded(i, feed)
        guarded(i - 1, down)

    for i in range(2 * PER):
        w, j = i // PER, i % PER
        sent(g_piece(w, j, x), g_ss.at[0, i])
        sent(g_piece(w, j, x), g_ss.at[1, i])
    for w in range(2):
        sent(g_piece(w, 0, xm), g_ss.at[2, w])
        sent(g_piece(w, 1, xp), g_ss.at[3, w])

    @pl.loop(0, NC)
    def _(k):
        sent(wdn.at[k, :, x], d_ss.at[k, 0])
        sent(wdn.at[k, :, x], d_ss.at[k, 1])
        sent(wdn.at[k, 0, xm], d_ss.at[k, 2])
        sent(wdn.at[k, 1, xp], d_ss.at[k, 3])
        sent(sb.at[k, pl.ds(0, NS - 1)], y2_ss.at[k])
        sent(rl2.at[k], f2_ss.at[k])
        sent(xb.at[k, pl.ds(0, NZ - 1)], r_ss.at[k])


def body(tokens, routes, route_weight, bias, w_gate, w_up, w_down):
    tok, feat = tokens.shape
    per, ff, _ = w_gate.shape
    experts = bias.shape[0]
    width = feat // NC
    rows = NS * PER * SLOTS
    meta = jnp.concatenate([routes.T.astype(F32), route_weight.T], axis=0)
    vmem, anywhere = pl.BlockSpec(memory_space=pltpu.VMEM), pl.BlockSpec(memory_space=pl.ANY)
    dma = pltpu.SemaphoreType.DMA
    mixed, counts, new_bias = pl.pallas_call(
        kernel,
        out_shape=(
            jax.ShapeDtypeStruct((tok, feat), BF16),
            jax.ShapeDtypeStruct((1, experts), jnp.int32),
            jax.ShapeDtypeStruct((1, experts), F32),
        ),
        in_specs=[vmem, vmem, anywhere, anywhere, anywhere, anywhere],
        out_specs=(vmem, vmem, vmem),
        scratch_shapes=[
            pltpu.VMEM((NC, NZ, tok, width), BF16),
            pltpu.VMEM((rows, NZ * tok), BF16),
            pltpu.VMEM((NZ, tok, rows), BF16),
            pltpu.VMEM((NZ, tok, rows), BF16),
            pltpu.VMEM((NC, NS, PER, SLOTS, width), BF16),
            pltpu.VMEM((NC, NS, PER, SLOTS, width), BF16),
            pltpu.VMEM((NC, NS, PER, SLOTS, width), BF16),
            pltpu.VMEM((2, per, NX, ff, feat), BF16),
            pltpu.VMEM((NC, per, NX, ff, width), BF16),
            pltpu.VMEM((per, NX, NS * SLOTS, ff), BF16),
            pltpu.VMEM((NC, 2, PER, SLOTS, width), BF16),
            pltpu.VMEM((NC, 2, PER, SLOTS, width), BF16),
            pltpu.VMEM((NC, 2, 4, tok, width), BF16),
            pltpu.VMEM((NZ, 16, tok), F32),
            pltpu.VMEM((NZ, NS * PER, tok), F32),
            pltpu.VMEM((NZ, NS * PER, tok), F32),
            pltpu.VMEM((5, 8, tok), F32),
            pltpu.VMEM((5, 8, tok), F32),
            dma((2,)),
            dma((NC,)),
            dma((NC,)),
            dma,
            dma,
            dma((5,)),
            dma((5,)),
            dma((NC,)),
            dma((NC, 2, 4)),
            dma((NC,)),
            dma((NC,)),
            dma((NC, 2)),
            dma((NC,)),
            dma((NC,)),
            dma((NC,)),
            dma((NC, 2)),
            dma((NC,)),
            dma((NC,)),
            dma((NC, 2, 4)),
            dma((4, 4)),
            dma((4, 4)),
            dma((NC, 4)),
            dma((NC, 4)),
        ],
        compiler_params=pltpu.CompilerParams(
            collective_id=0, has_side_effects=True, vmem_limit_bytes=67_043_328
        ),
        name="moe_layer",
    )(meta, bias.reshape(1, experts), tokens, w_gate, w_up, w_down)
    return mixed, new_bias.reshape(experts), counts.reshape(experts)


def solution(mesh):
    torus = Mesh(mesh.devices.reshape(NX, NY, NZ, NCORE), DP_EXPERT)
    placed = (
        P(DP_EXPERT, None),
        P(DP_EXPERT, None),
        P(DP_EXPERT, None),
        P(),
        P(EXPERT, "dp", None),
        P(EXPERT, "dp", None),
        P(EXPERT, "dp", None),
    )
    return jax.shard_map(
        body, mesh=torus, in_specs=placed, out_specs=(P(DP_EXPERT, None), P(), P()), check_vma=False
    )
```

time: 427 us -> 228 us (0.53); the launches traced: 419 us -> 227 us
  Pallas kernels: 0 us -> 221 us
  waiting for transfers between devices: 141 us -> 0 us
  local copies, waits for them, and re-layouts: 85.4 us -> 4.17 us
  blocking collectives: 71 us -> 0 us
  starting transfers between devices: 37.6 us -> 0 us
  matrix products: 35.2 us -> 0 us
  other arithmetic: 33.6 us -> 1.98 us
  between operations: 14.8 us -> 0.64 us
    pallas_call x0 -> x1, Pallas kernels: none -> 221 us  [body(): pl.pallas_call(kernel, out_shape=(jax.ShapeDtypeStruct((tok, feat), BF16)...]
    all_to_all x4 -> x0, waiting for transfers between devices: 92.5 us -> none  [the longest x2 53.8 us: grouped_exchange(): lax.all_to_all(group, axis, split_axis=split_dim, concat_axis=concat_dim,...]
    psum x4 -> x0, blocking collectives: 71 us -> none  [over_axes(): array = lax.psum(array, axis)]
    all_gather x1 -> x0, waiting for transfers between devices: 48.9 us -> none  [sent_together(): whole, at, outs = (lax.all_gather(both, axis, axis=dim, tiled=True), 0, [])]
    all_to_all x4 -> x0, starting transfers between devices: 37.6 us -> none  [the longest x2 19.5 us: grouped_exchange(): lax.all_to_all(group, axis, split_axis=split_dim, concat_axis=concat_dim,...]
    dot_general x6 -> x0, matrix products: 35.2 us -> none  [the longest x2 13.3 us: expert_products(): jnp.einsum('sjcd,jfd->sjcf', received, gate_w, preferred_element_type=jnp...]
    gather x3 -> x0, local copies, waits for them, and re-layouts: 28.1 us -> none  [the longest x2 16 us: body(): tokens[source]]
    slice x3 -> x0, local copies, waits for them, and re-layouts: 18.8 us -> none  [grouped_exchange(): lax.slice_in_dim(a, k * (items // count), (k + 1) * (items // count), axi...]
  transfers between devices with their start and end apart: 5 -> 0, of which waited for: 3 -> 0; matrix products, arithmetic and copies ran while one was open for 23% -> 0% of each run, Pallas kernels for 0% -> 0%
where the time goes in v1:
time: 228 us; the launch traced here: 227 us
  Pallas kernels  221 us (97%)
  local copies, waits for them, and re-layouts  4.17 us (2%)
    pallas_call x1, Pallas kernels, body(): pl.pallas_call(kernel, out_shape=(jax.ShapeDtypeStruct((tok, feat), BF16)...  221 us

profile of v1, /device:TPU:8, one launch (start us, length us, event | category | flops | bytes accessed | tf_op | source)
XLA Modules:
  0.0 227.3 jit_solution(2641105761814734316)
XLA Ops:
  0.6 0.7 convert_bitcast_fusion
  1.3 1.3 pad_maximum_fusion.meta_ref
  2.6 220.5 %moe_layer.1 = (bf16[128,2048]{1,0:T(8,128)(2,1)}, s32[1,128]{1,0:T(1,128)}, f32[1,128]{1,0:T(1,128)}) custom-call(f32[16,128]{1,0:T(8,128)} %pad_maximum_fusion.meta_ref, f32[1,128]{1,0:T(1,128)} %bitcast.7, bf16[128,2048]{1,0:T(8,128)(2,1)} %tok_ref.1, bf16[2,192,2048]{2,1,0:T(8,128)(2,1)} %wg_ref.1, bf16[2,192,2048]{2,1,0:T(8,128)(2,1)} %wu_ref.1, ...), custom_call_target="tpu_custom_call" | custom-call | tf_op jit(solution)/shard_map/moe_layer/pallas_call | solution.py:427
  223.1 1.9 copy.13
  225.0 1.2 copy.14
  226.2 1.1 copy.15

commit v2 on v1

v2 whole, which is shorter than its diff:
```python
import functools

import jax
import jax.numpy as jnp
from jax import lax
from jax.experimental import pallas as pl
from jax.experimental.pallas import tpu as pltpu
from jax.sharding import Mesh
from jax.sharding import PartitionSpec as P

EXPERT = ("expert_0", "expert_1", "expert_2")
DP_EXPERT = ("dp", "expert_0", "expert_1", "expert_2")
MESH = pl.DeviceIdType.MESH
BF16, F32 = jnp.bfloat16, jnp.float32

NX, NY, NZ, NCORE = 4, 4, 8, 2
PER = 2
CAP = 10
NS = NY * NCORE
SLOTS = CAP * NZ
NC = 8
bias_rate = 0.05

NT = (((1,), (1,)), ((), ()))


def wrap(v, n):
    return lax.rem(v + 2 * n, n)


def kernel(
    route_ref, weight_ref, tok_ref, wg_ref, wu_ref, wd_ref,
    out_ref, cnt_ref,
    xb, pm, wh, wl, sb, rb, cb, wgu, wdn, hid, rl1, rl2, rsb, mroute, mweight, keys, wks, csend, crecv, outb,
    loc_s, tok_s, wdl_s, out_s, meta_ss, meta_rs, c_ss, c_rs,
    z_ss, z_rs, y1_ss, y1_rs, l1_rs, f1_ss, y2_ss, y2_rs, l2_rs, f2_ss, r_ss, r_rs,
    g_ss, g_rs, d_ss, d_rs,
):
    x, y = lax.axis_index("dp"), lax.axis_index("expert_0")
    z, c = lax.axis_index("expert_1"), lax.axis_index("expert_2")
    feat = tok_ref.shape[1]
    width = feat // NC
    tok = tok_ref.shape[0]
    ff = wg_ref.shape[1]
    xp, xm = wrap(x + 1, NX), wrap(x - 1, NX)
    yp, ym = wrap(y + 1, NY), wrap(y - 1, NY)
    other = 1 - c
    mine = y * NCORE + c
    home = (x, y, z, c)

    def rcopy(src, dst, ss, rs, to):
        return pltpu.make_async_remote_copy(
            src_ref=src, dst_ref=dst, send_sem=ss, recv_sem=rs, device_id=to, device_id_type=MESH
        )

    def got(ref, sem):
        rcopy(ref, ref, sem, sem, (xp, y, z, c)).wait_recv()

    def sent(ref, sem):
        rcopy(ref, ref, sem, sem, (xp, y, z, c)).wait_send()

    own_g = [
        pltpu.make_async_copy(wg_ref, wgu.at[0, :, x], loc_s.at[0]),
        pltpu.make_async_copy(wu_ref, wgu.at[1, :, x], loc_s.at[1]),
    ]
    own_g[0].start()
    own_g[1].start()

    def columns(k):
        return pl.ds(pl.multiple_of(k * width, width), width)

    def tok_copy(k):
        return pltpu.make_async_copy(tok_ref.at[:, columns(k)], xb.at[k, z], tok_s.at[(k + NC - 1) // NC])

    def wd_copy(k):
        return pltpu.make_async_copy(wd_ref.at[:, :, columns(k)], wdn.at[k, :, x], wdl_s)

    @pl.loop(0, NC)
    def _(k):
        tok_copy(k).start()

    @pl.loop(0, NC)
    def _(k):
        wd_copy(k).start()

    barrier = pltpu.get_barrier_semaphore()
    peers = [(xp, y, z, c), (xm, y, z, c), (x, y, z, other)]
    peers += [(x, yy, z, cc) for yy in (yp, ym) for cc in range(NCORE)]
    peers += [(x, y, wrap(z + 1, NZ), c), (x, y, wrap(z - 1, NZ), c)]
    for p in peers:
        pl.semaphore_signal(barrier, inc=1, device_id=p, device_id_type=MESH)
    pl.semaphore_wait(barrier, len(peers))

    def g_piece(w, j, xs):
        return wgu.at[w, j, xs]

    def g_own(w, j):
        a = g_piece(w, j, x)
        rcopy(a, a, g_ss, g_rs.at[w, j, 0], (xp, y, z, c)).start()
        rcopy(a, a, g_ss, g_rs.at[w, j, 0], (xm, y, z, c)).start()

    def g_arrived(w, j):
        got(wgu.at[w, :, x], g_rs.at[w, j, 0])

    def halves(ref):
        rows = ref.shape[0] // 2
        return ref.at[pl.ds(0, rows)], ref.at[pl.ds(rows, rows)]

    def g_relay(w, j):
        g_arrived(w, j)
        a = halves(g_piece(w, j, xm))[0]
        rcopy(a, a, g_ss, g_rs.at[w, j, 1], (xp, y, z, c)).start()
        b = halves(g_piece(w, j, xp))[1]
        rcopy(b, b, g_ss, g_rs.at[w, j, 1], (xm, y, z, c)).start()

    own_g[0].wait()
    g_own(0, 0)
    own_g[1].wait()
    g_own(1, 0)

    def z_hop(k, h):
        s = 1 - 2 * lax.rem(k, 2)
        far = xb.at[k, wrap(z - s * (h - 1), NZ)]
        near = xb.at[k, wrap(z + s * (h - 1), NZ)]
        if h >= 2:
            got(xb.at[k, pl.ds(0, 2)], z_rs.at[k, h - 2])
        rcopy(far, far, z_ss, z_rs.at[k, h - 1], (x, y, wrap(z + s, NZ), c)).start()
        if h < 4:
            rcopy(near, near, z_ss, z_rs.at[k, h - 1], (x, y, wrap(z - s, NZ), c)).start()

    def m_hop(h):
        for a, (own, held) in enumerate(((route_ref, mroute), (weight_ref, mweight))):
            if h >= 2:
                got(held.at[pl.ds(0, 2)], meta_rs.at[a, h - 2])
            p, q = wrap(z - (h - 1), NZ), wrap(z + (h - 1), NZ)
            rcopy(
                own if h == 1 else held.at[p], held.at[p], meta_ss.at[a], meta_rs.at[a, h - 1],
                (x, y, wrap(z + 1, NZ), c),
            ).start()
            if h < 4:
                rcopy(
                    own if h == 1 else held.at[q], held.at[q], meta_ss.at[a], meta_rs.at[a, h - 1],
                    (x, y, wrap(z - 1, NZ), c),
                ).start()

    m_hop(1)
    mroute[z] = route_ref[...]
    mweight[z] = weight_ref[...]
    tok_copy(0).wait()
    z_hop(0, 1)
    m_hop(2)
    m_hop(3)
    got(xb.at[pl.ds(0, NC - 1), z], tok_s.at[1])
    z_hop(1, 1)
    m_hop(4)

    got(mroute.at[0], meta_rs.at[0, 3])
    got(mweight.at[0], meta_rs.at[1, 3])
    row = lax.broadcasted_iota(jnp.int32, (NS * PER, tok), 0)
    expert = (row // 4) * (NZ * 4) + z * 4 + row % 4
    before = (
        lax.broadcasted_iota(jnp.int32, (tok, tok), 0)
        < lax.broadcasted_iota(jnp.int32, (tok, tok), 1)
    ).astype(F32).astype(BF16)
    slot_row = lax.broadcasted_iota(jnp.int32, (NS * PER, SLOTS, tok), 1).astype(F32)

    @pl.loop(0, NZ)
    def _(b):
        hit = jnp.zeros((NS * PER, tok), F32)
        weight = jnp.zeros((NS * PER, tok), F32)
        for k in range(8):
            same = mroute[b, k : k + 1, :] == expert
            hit = jnp.where(same, 1.0, hit)
            weight = jnp.where(same, mweight[b, k : k + 1, :], weight)
        rank = jnp.dot(hit.astype(BF16), before, preferred_element_type=F32)
        key = jnp.where(hit > 0.0, rank * NZ + b.astype(F32), -1.0)
        keys[b] = key
        wks[b] = weight
        pick = jnp.where(key[:, None, :] == slot_row, 1.0, 0.0)
        at = pl.ds(pl.multiple_of(b * tok, tok), tok)
        pm[:, at] = pick.reshape(NS * PER * SLOTS, tok).astype(BF16)

    def y_send(src, dst, rl, ss, rs, ls):
        rcopy(src(y * NCORE + other), dst(mine), ss, rs, (x, y, z, other)).start()
        for cc, yf in ((0, yp), (1, ym)):
            opp = wrap(y + 2, NY)
            rcopy(src(opp * NCORE + cc), rl(cc), ss, ls, (x, yf, z, c)).start()
        for yy in (yp, ym):
            for cc in range(NCORE):
                rcopy(src(yy * NCORE + cc), dst(mine), ss, rs, (x, yy, z, cc)).start()

    def y_forward(dst, rl, landed, fs, rs, ls):
        got(landed, ls)
        rcopy(rl(0), dst(ym * NCORE + c), fs, rs, (x, yp, z, 0)).start()
        rcopy(rl(1), dst(yp * NCORE + c), fs, rs, (x, ym, z, 1)).start()

    def pick_rows(k):
        got(xb.at[k, 0], z_rs.at[k, 3])
        half = NS * PER * SLOTS // 2

        @pl.loop(0, 2)
        def _(p):
            rows = pm[pl.ds(pl.multiple_of(p * half, half), half), :]
            picked = jnp.dot(rows, xb[k].reshape(NZ * tok, width), preferred_element_type=F32)
            picked = picked.astype(BF16).reshape(NS // 2, PER, SLOTS, width)
            sb[k, pl.ds(p * (NS // 2), NS // 2)] = picked

        rb[k, mine] = sb[k, mine]
        y_send(
            lambda d: sb.at[k, d], lambda d: rb.at[k, d], lambda d: rl1.at[k, d],
            y1_ss, y1_rs.at[k], l1_rs.at[k],
        )

    def pass_rows(k):
        y_forward(
            lambda d: rb.at[k, d], lambda d: rl1.at[k, d], rl1.at[k], f1_ss, y1_rs.at[k], l1_rs.at[k]
        )

    def guarded(k, fn, first=0, last=NC):
        @pl.when(jnp.logical_and(k >= first, k < last))
        def _():
            fn(k)

    units, early = 2 * NC, NC // 2

    def unit(u):
        late = u // NC
        k = (1 - late) * (u % early) + late * (early + (u - NC + units) % NC // 2)
        j = (1 - late) * (u // early) + late * (u % 2)
        return k, j

    def d_own(u):
        k, j = unit(u)
        a = wdn.at[k, j, x]
        rcopy(a, a, d_ss, d_rs.at[u, 0], (xp, y, z, c)).start()
        rcopy(a, a, d_ss, d_rs.at[u, 0], (xm, y, z, c)).start()

    def d_relay(u):
        k, j = unit(u)
        got(wdn.at[k, :, x], d_rs.at[u, 0])
        a = halves(wdn.at[k, j, xm])[0]
        rcopy(a, a, d_ss, d_rs.at[u, 1], (xp, y, z, c)).start()
        b = halves(wdn.at[k, j, xp])[1]
        rcopy(b, b, d_ss, d_rs.at[u, 1], (xm, y, z, c)).start()

    expert_row = lax.broadcasted_iota(jnp.int32, (tok, tok), 0)

    def count(b, total):
        hit = jnp.zeros((tok, tok), F32)
        for k in range(8):
            hit = jnp.where(mroute[b, k : k + 1, :] == expert_row, 1.0, hit)
        ones = jnp.ones((8, tok), BF16)
        return total + lax.dot_general(ones, hit.astype(BF16), NT, preferred_element_type=F32)

    y1 = y + 1 - 2 * lax.rem(y, 2)
    x1 = x + 1 - 2 * lax.rem(x, 2)
    partners = [(x, y, z, other), (x, y1, z, c), (x, NY - 1 - y, z, c), (x1, y, z, c), (NX - 1 - x, y, z, c)]

    def c_move(s):
        return rcopy(csend.at[s], crecv.at[s], c_ss.at[s], c_rs.at[s], partners[s])

    def c_step(s):
        if s > 0:
            c_move(s - 1).wait()
            total = csend[s - 1] + crecv[s - 1]
        if s == len(partners):
            cnt_ref[...] = total[0:1]
            return
        if s > 0:
            csend[s] = total
        c_move(s).start()

    def weigh(b):
        same = keys[b][:, None, :] == slot_row
        placed = jnp.where(same, wks[b][:, None, :], 0.0).reshape(NS * PER * SLOTS, tok).T
        high = placed.astype(BF16)
        wh[b] = high
        wl[b] = (placed - high.astype(F32)).astype(BF16)

    @pl.loop(0, NC + 4)
    def _(i):
        guarded(i - 2, lambda k: z_hop(k, 4))
        guarded(i - 1, lambda k: z_hop(k, 3))
        guarded(i, lambda k: z_hop(k, 2))
        guarded(i + 2, lambda k: z_hop(k, 1))
        guarded(i - 3, pick_rows)
        guarded(i - 4, pass_rows)

        @pl.when(i == 3)
        def _():
            g_relay(0, 0)

        @pl.when(i == 5)
        def _():
            g_relay(1, 0)

        @pl.when(i == 6)
        def _():
            got(wdn.at[:, :, x], wdl_s)
            for u in range(early):
                d_own(u)
            g_own(0, 1)

        @pl.when(i == 10)
        def _():
            for u in range(early):
                d_relay(u)
            g_own(1, 1)

        guarded(i - 4, weigh)

        @pl.when(i == 4)
        def _():
            csend[0] = lax.fori_loop(0, NZ, count, jnp.zeros((8, tok), F32))

        for s, at in enumerate((5, 6, 8, 11)):

            @pl.when(i == at)
            def _(s=s):
                c_step(s)

    @pl.loop(0, NC)
    def _(k):
        got(rb.at[k, pl.ds(0, NS - 1)], y1_rs.at[k])

    sent(xb.at[:, pl.ds(0, NZ - 1)], z_ss)
    sent(sb.at[:, pl.ds(0, NS - 1)], y1_ss)
    sent(rl1, f1_ss)
    sent(mroute.at[pl.ds(0, NZ - 1)], meta_ss.at[0])
    sent(mweight.at[pl.ds(0, NZ - 1)], meta_ss.at[1])

    def hidden_of(j, xs):
        @pl.loop(0, 2)
        def _(t):
            part = pl.ds(t * (NS // 2), NS // 2)
            gate = up = None
            for k in range(NC):
                rows = rb[k, part, j].reshape(NS // 2 * SLOTS, width)
                cols = slice(k * width, (k + 1) * width)
                g = lax.dot_general(rows, wgu[0, j, xs, :, cols], NT, preferred_element_type=F32)
                u = lax.dot_general(rows, wgu[1, j, xs, :, cols], NT, preferred_element_type=F32)
                gate = g if gate is None else gate + g
                up = u if up is None else up + u
            act = (gate / (1.0 + jnp.exp(-gate)) * up).astype(BF16)
            half = NS // 2 * SLOTS
            hid[j, xs, pl.ds(pl.multiple_of(t * half, half), half), :] = act

    opposite = wrap(x + 2, NX)

    def g_relayed(j):
        for w in range(2):
            got(g_piece(w, j, opposite), g_rs.at[w, j, 1])

    g_relay(0, 1)
    g_relayed(0)

    @pl.loop(0, NX)
    def _(xs):
        hidden_of(0, xs)

    def second_expert():
        @pl.loop(0, NX - 1)
        def _(step):
            hidden_of(1, wrap(x + 3 + step, NX))

        d_relay(early)
        d_own(early + 1)
        d_own(early + 2)
        g_relayed(1)
        hidden_of(1, opposite)

    def down(u):
        k, j = unit(u)
        got(wdn.at[k, j, opposite], d_rs.at[u, 1])
        total = None
        for xs in range(NX):
            t = jnp.dot(hid[j, xs], wdn[k, j, xs], preferred_element_type=F32)
            total = t if total is None else total + t
        sb[k, :, j] = total.astype(BF16).reshape(NS, SLOTS, width)
        cb[k, mine, j] = sb[k, mine, j]
        y_send(
            lambda d: sb.at[k, d, j], lambda d: cb.at[k, d, j], lambda d: rl2.at[k, d, j],
            y2_ss, y2_rs.at[k, j], l2_rs.at[k, j],
        )

    def pass_back(u):
        k, j = unit(u)
        y_forward(
            lambda d: cb.at[k, d, j], lambda d: rl2.at[k, d, j], rl2.at[k, :, j],
            f2_ss, y2_rs.at[k, j], l2_rs.at[k, j],
        )

    def r_hop(k, h):
        s = 1 - 2 * lax.rem(k, 2)
        if h >= 2:
            got(rsb.at[k, :, h - 2], r_rs.at[k, h - 2])
        for way, t, step in ((0, z + (5 - h) * s, s), (1, z - (4 - h) * s, -s)):
            if h == 4 and way == 1:
                continue
            t = wrap(t, NZ)
            if h >= 2:
                xb[k, t] = (xb[k, t].astype(F32) + rsb[k, way, h - 2].astype(F32)).astype(BF16)
            to = (x, y, wrap(z + step, NZ), c)
            rcopy(xb.at[k, t], rsb.at[k, way, h - 1], r_ss, r_rs.at[k, h - 1], to).start()

    def combine(k):
        for j in range(PER):
            got(cb.at[k, pl.ds(0, NS - 1), j], y2_rs.at[k, j])

        @pl.loop(0, 2)
        def _(p):
            part = pl.ds(p * (NZ // 2), NZ // 2)
            served = cb[k].reshape(NS * PER * SLOTS, width)
            hi = wh[part].reshape(NZ // 2 * tok, NS * PER * SLOTS)
            lo = wl[part].reshape(NZ // 2 * tok, NS * PER * SLOTS)
            summed = jnp.dot(hi, served, preferred_element_type=F32)
            summed += jnp.dot(lo, served, preferred_element_type=F32)
            xb[k, part] = summed.astype(BF16).reshape(NZ // 2, tok, width)

        r_hop(k, 1)

    def out_copy(k):
        return pltpu.make_async_copy(outb.at[k], out_ref.at[:, columns(k)], out_s)

    def finish(k):
        got(rsb.at[k, 0, 3], r_rs.at[k, 3])
        value = xb[k, z].astype(F32) + rsb[k, 0, 3].astype(F32) + rsb[k, 1, 2].astype(F32)
        outb[k] = value.astype(BF16)
        out_copy(k).start()

    def completed(u, fn):
        k, j = unit(u)

        @pl.when(jnp.logical_and(jnp.logical_and(u >= early, u < units), j == 1))
        def _():
            fn(k)

    @pl.loop(0, units + 12)
    def _(i):
        guarded(i - 2, pass_back, 0, units)
        completed(i - 12, finish)
        completed(i - 10, lambda k: r_hop(k, 4))
        completed(i - 8, lambda k: r_hop(k, 3))
        completed(i - 6, lambda k: r_hop(k, 2))
        completed(i - 4, combine)

        @pl.when(i == early - 1)
        def _():
            d_own(early)
            g_relay(1, 1)

        @pl.when(i == early)
        def _():
            second_expert()

        guarded(i + 1, d_relay, early + 1, units)
        guarded(i + 3, d_own, early + 3, units)
        guarded(i, down, 0, units)

        @pl.when(i == early + 2)
        def _():
            c_step(4)

        @pl.when(i == units - 2)
        def _():
            c_step(5)

    sent(wgu.at[:, :, pl.ds(0, NX - 1)], g_ss)
    sent(wdn.at[:, :, pl.ds(0, NX - 1)], d_ss)
    sent(sb.at[:, pl.ds(0, NS - 1)], y2_ss)
    sent(rl2, f2_ss)
    sent(xb.at[:, pl.ds(0, NZ - 1)], r_ss)
    got(outb, out_s)


def close(mean_load, experts, mixed_ref, total_ref, bias_ref, out_ref, new_bias_ref, count_ref):
    out_ref[...] = mixed_ref[...]
    totals = total_ref[...]
    over = mean_load - experts * totals
    sign = jnp.where(over > 0.0, 1.0, jnp.where(over < 0.0, -1.0, 0.0))
    new_bias_ref[...] = bias_ref[...] + bias_rate * sign
    count_ref[...] = totals.astype(jnp.int32)


def body(tokens, routes, route_weight, bias, w_gate, w_up, w_down):
    tok, feat = tokens.shape
    per, ff, _ = w_gate.shape
    experts = bias.shape[0]
    width = feat // NC
    rows = NS * PER * SLOTS
    vmem, anywhere = pl.BlockSpec(memory_space=pltpu.VMEM), pl.BlockSpec(memory_space=pl.ANY)
    dma = pltpu.SemaphoreType.DMA
    mixed, totals = pl.pallas_call(
        kernel,
        out_shape=(
            jax.ShapeDtypeStruct((tok, feat), BF16),
            jax.ShapeDtypeStruct((1, experts), F32),
        ),
        in_specs=[vmem, vmem, anywhere, anywhere, anywhere, anywhere],
        out_specs=(anywhere, vmem),
        scratch_shapes=[
            pltpu.VMEM((NC, NZ, tok, width), BF16),
            pltpu.VMEM((rows, NZ * tok), BF16),
            pltpu.VMEM((NZ, tok, rows), BF16),
            pltpu.VMEM((NZ, tok, rows), BF16),
            pltpu.VMEM((NC, NS, PER, SLOTS, width), BF16),
            pltpu.VMEM((NC, NS, PER, SLOTS, width), BF16),
            pltpu.VMEM((NC, NS, PER, SLOTS, width), BF16),
            pltpu.VMEM((2, per, NX, ff, feat), BF16),
            pltpu.VMEM((NC, per, NX, ff, width), BF16),
            pltpu.VMEM((per, NX, NS * SLOTS, ff), BF16),
            pltpu.VMEM((NC, 2, PER, SLOTS, width), BF16),
            pltpu.VMEM((NC, 2, PER, SLOTS, width), BF16),
            pltpu.VMEM((NC, 2, 4, tok, width), BF16),
            pltpu.VMEM((NZ, 8, tok), jnp.int32),
            pltpu.VMEM((NZ, 8, tok), F32),
            pltpu.VMEM((NZ, NS * PER, tok), F32),
            pltpu.VMEM((NZ, NS * PER, tok), F32),
            pltpu.VMEM((5, 8, tok), F32),
            pltpu.VMEM((5, 8, tok), F32),
            pltpu.VMEM((NC, tok, width), BF16),
            dma((2,)),
            dma((2,)),
            dma,
            dma,
            dma((2,)),
            dma((2, 4)),
            dma((5,)),
            dma((5,)),
            dma,
            dma((NC, 4)),
            dma,
            dma((NC,)),
            dma((NC,)),
            dma,
            dma,
            dma((NC, PER)),
            dma((NC, PER)),
            dma,
            dma,
            dma((NC, 4)),
            dma,
            dma((2, PER, 2)),
            dma,
            dma((2 * NC, 2)),
        ],
        compiler_params=pltpu.CompilerParams(
            collective_id=0, has_side_effects=True, vmem_limit_bytes=67_043_328
        ),
        name="moe_layer",
    )(routes.T, route_weight.T, tokens, w_gate, w_up, w_down)
    everyone = NX * NY * NZ * NCORE
    mixed, new_bias, counts = pl.pallas_call(
        functools.partial(close, float(tok * routes.shape[1] * everyone), float(experts)),
        out_shape=(
            jax.ShapeDtypeStruct((tok, feat), BF16),
            jax.ShapeDtypeStruct((1, experts), F32),
            jax.ShapeDtypeStruct((1, experts), jnp.int32),
        ),
        in_specs=[vmem] * 3,
        out_specs=(vmem,) * 3,
        name="moe_close",
    )(mixed, totals, bias.reshape(1, experts))
    return mixed, new_bias.reshape(experts), counts.reshape(experts)


def solution(mesh):
    torus = Mesh(mesh.devices.reshape(NX, NY, NZ, NCORE), DP_EXPERT)
    placed = (
        P(DP_EXPERT, None),
        P(DP_EXPERT, None),
        P(DP_EXPERT, None),
        P(),
        P(EXPERT, "dp", None),
        P(EXPERT, "dp", None),
        P(EXPERT, "dp", None),
    )
    return jax.shard_map(
        body, mesh=torus, in_specs=placed, out_specs=(P(DP_EXPERT, None), P(), P()), check_vma=False
    )
```

time: 228 us -> 204 us (0.89)
  Pallas kernels: 221 us -> 202 us
  local copies, waits for them, and re-layouts: 4.17 us -> 0 us
    pallas_call x1, Pallas kernels: 221 us -> 201 us  [body(): pl.pallas_call(kernel, out_shape=(jax.ShapeDtypeStruct((tok, feat), BF16)...]
    unnamed x3 -> x0, local copies, waits for them, and re-layouts: 4.17 us -> none
where the time goes in v2:
time: 204 us; the launch traced here: 203 us
  Pallas kernels  202 us (99%)
    pallas_call x1, Pallas kernels, body(): pl.pallas_call(kernel, out_shape=(jax.ShapeDtypeStruct((tok, feat), BF16)...  201 us

profile of v2, /device:TPU:8, one launch (start us, length us, event | category | flops | bytes accessed | tf_op | source)
XLA Modules:
  0.0 203.1 jit_solution(15711233826497591857)
XLA Ops:
  0.6 200.5 %moe_layer.1 = (bf16[128,2048]{1,0:T(8,128)(2,1)}, f32[1,128]{1,0:T(1,128)}) custom-call(s32[8,128]{1,0:T(8,128)} %bitcast.5, f32[8,128]{1,0:T(8,128)} %bitcast.6, bf16[128,2048]{1,0:T(8,128)(2,1)} %tok_ref.1, bf16[2,192,2048]{2,1,0:T(8,128)(2,1)} %wg_ref.1, bf16[2,192,2048]{2,1,0:T(8,128)(2,1)} %wu_ref.1, bf16[2,192,2048]{2,1,0:T(8,128)(2,1)} %wd_ref.1), custom_call_target="tpu_custom_call" | custom-call | tf_op jit(solution)/shard_map/moe_layer/pallas_call | solution.py:493
  201.2 1.9 moe_close.1

commit v3 on v2

--- a/solution.py
+++ b/solution.py
@@ -18,7 +18,9 @@
 CAP = 10
 NS = NY * NCORE
 SLOTS = CAP * NZ
+SPAN = 32
 NC = 8
+PARTS = 2
 bias_rate = 0.05
 
 NT = (((1,), (1,)), ((), ()))
@@ -31,7 +33,7 @@
 def kernel(
     route_ref, weight_ref, tok_ref, wg_ref, wu_ref, wd_ref,
     out_ref, cnt_ref,
-    xb, pm, wh, wl, sb, rb, cb, wgu, wdn, hid, rl1, rl2, rsb, mroute, mweight, keys, wks, csend, crecv, outb,
+    xb, pm, ws, sb, rb, cb, wgu, wdn, hid, rl1, rl2, rsb, mroute, mweight, keys, wks, csend, crecv, outb,
     loc_s, tok_s, wdl_s, out_s, meta_ss, meta_rs, c_ss, c_rs,
     z_ss, z_rs, y1_ss, y1_rs, l1_rs, f1_ss, y2_ss, y2_rs, l2_rs, f2_ss, r_ss, r_rs,
     g_ss, g_rs, d_ss, d_rs,
@@ -40,6 +42,7 @@
     z, c = lax.axis_index("expert_1"), lax.axis_index("expert_2")
     feat = tok_ref.shape[1]
     width = feat // NC
+    thin = width // PARTS
     tok = tok_ref.shape[0]
     ff = wg_ref.shape[1]
     xp, xm = wrap(x + 1, NX), wrap(x - 1, NX)
@@ -173,24 +176,25 @@
             hit = jnp.where(same, 1.0, hit)
             weight = jnp.where(same, mweight[b, k : k + 1, :], weight)
         rank = jnp.dot(hit.astype(BF16), before, preferred_element_type=F32)
-        key = jnp.where(hit > 0.0, rank * NZ + b.astype(F32), -1.0)
+        key = jnp.where(jnp.logical_and(hit > 0.0, rank < CAP), b.astype(F32) * CAP + rank, -1.0)
         keys[b] = key
         wks[b] = weight
         pick = jnp.where(key[:, None, :] == slot_row, 1.0, 0.0)
         at = pl.ds(pl.multiple_of(b * tok, tok), tok)
         pm[:, at] = pick.reshape(NS * PER * SLOTS, tok).astype(BF16)
 
-    def y_send(src, dst, rl, ss, rs, ls):
+    def y_far(src, rl, ss, ls):
+        opp = wrap(y + 2, NY)
+        for cc, yf in ((0, yp), (1, ym)):
+            rcopy(src(opp * NCORE + cc), rl(cc), ss, ls, (x, yf, z, c)).start()
+
+    def y_send(src, dst, ss, rs):
         rcopy(src(y * NCORE + other), dst(mine), ss, rs, (x, y, z, other)).start()
-        for cc, yf in ((0, yp), (1, ym)):
-            opp = wrap(y + 2, NY)
-            rcopy(src(opp * NCORE + cc), rl(cc), ss, ls, (x, yf, z, c)).start()
         for yy in (yp, ym):
             for cc in range(NCORE):
                 rcopy(src(yy * NCORE + cc), dst(mine), ss, rs, (x, yy, z, cc)).start()
 
-    def y_forward(dst, rl, landed, fs, rs, ls):
-        got(landed, ls)
+    def y_forward(dst, rl, fs, rs):
         rcopy(rl(0), dst(ym * NCORE + c), fs, rs, (x, yp, z, 0)).start()
         rcopy(rl(1), dst(yp * NCORE + c), fs, rs, (x, ym, z, 1)).start()
 
@@ -206,42 +210,29 @@
             sb[k, pl.ds(p * (NS // 2), NS // 2)] = picked
 
         rb[k, mine] = sb[k, mine]
-        y_send(
-            lambda d: sb.at[k, d], lambda d: rb.at[k, d], lambda d: rl1.at[k, d],
-            y1_ss, y1_rs.at[k], l1_rs.at[k],
-        )
+        y_far(lambda d: sb.at[k, d], lambda d: rl1.at[k, d], y1_ss, l1_rs.at[k])
+        y_send(lambda d: sb.at[k, d], lambda d: rb.at[k, d], y1_ss, y1_rs.at[k])
 
     def pass_rows(k):
-        y_forward(
-            lambda d: rb.at[k, d], lambda d: rl1.at[k, d], rl1.at[k], f1_ss, y1_rs.at[k], l1_rs.at[k]
-        )
+        got(rl1.at[k], l1_rs.at[k])
+        y_forward(lambda d: rb.at[k, d], lambda d: rl1.at[k, d], f1_ss, y1_rs.at[k])
 
     def guarded(k, fn, first=0, last=NC):
         @pl.when(jnp.logical_and(k >= first, k < last))
         def _():
             fn(k)
 
-    units, early = 2 * NC, NC // 2
-
-    def unit(u):
-        late = u // NC
-        k = (1 - late) * (u % early) + late * (early + (u - NC + units) % NC // 2)
-        j = (1 - late) * (u // early) + late * (u % 2)
-        return k, j
-
-    def d_own(u):
-        k, j = unit(u)
+    def d_own(k, j):
         a = wdn.at[k, j, x]
-        rcopy(a, a, d_ss, d_rs.at[u, 0], (xp, y, z, c)).start()
-        rcopy(a, a, d_ss, d_rs.at[u, 0], (xm, y, z, c)).start()
-
-    def d_relay(u):
-        k, j = unit(u)
-        got(wdn.at[k, :, x], d_rs.at[u, 0])
+        rcopy(a, a, d_ss, d_rs.at[k, j, 0], (xp, y, z, c)).start()
+        rcopy(a, a, d_ss, d_rs.at[k, j, 0], (xm, y, z, c)).start()
+
+    def d_relay(k, j):
+        got(wdn.at[k, :, x], d_rs.at[k, j, 0])
         a = halves(wdn.at[k, j, xm])[0]
-        rcopy(a, a, d_ss, d_rs.at[u, 1], (xp, y, z, c)).start()
+        rcopy(a, a, d_ss, d_rs.at[k, j, 1], (xp, y, z, c)).start()
         b = halves(wdn.at[k, j, xp])[1]
-        rcopy(b, b, d_ss, d_rs.at[u, 1], (xm, y, z, c)).start()
+        rcopy(b, b, d_ss, d_rs.at[k, j, 1], (xm, y, z, c)).start()
 
     expert_row = lax.broadcasted_iota(jnp.int32, (tok, tok), 0)
 
@@ -270,12 +261,15 @@
             csend[s] = total
         c_move(s).start()
 
+    span_row = lax.broadcasted_iota(jnp.int32, (NS * PER, SPAN, tok), 1)
+
     def weigh(b):
-        same = keys[b][:, None, :] == slot_row
-        placed = jnp.where(same, wks[b][:, None, :], 0.0).reshape(NS * PER * SLOTS, tok).T
+        pair = b // 2
+        same = keys[b][:, None, :] == (span_row + 16 * pair).astype(F32)
+        placed = jnp.where(same, wks[b][:, None, :], 0.0).reshape(NS * PER * SPAN, tok).T
         high = placed.astype(BF16)
-        wh[b] = high
-        wl[b] = (placed - high.astype(F32)).astype(BF16)
+        ws[pair, 0, b % 2] = high
+        ws[pair, 1, b % 2] = (placed - high.astype(F32)).astype(BF16)
 
     @pl.loop(0, NC + 4)
     def _(i):
@@ -293,19 +287,12 @@
         @pl.when(i == 5)
         def _():
             g_relay(1, 0)
-
-        @pl.when(i == 6)
-        def _():
-            got(wdn.at[:, :, x], wdl_s)
-            for u in range(early):
-                d_own(u)
             g_own(0, 1)
+            g_own(1, 1)
 
         @pl.when(i == 10)
         def _():
-            for u in range(early):
-                d_relay(u)
-            g_own(1, 1)
+            g_relay(0, 1)
 
         guarded(i - 4, weigh)
 
@@ -351,117 +338,123 @@
         for w in range(2):
             got(g_piece(w, j, opposite), g_rs.at[w, j, 1])
 
-    g_relay(0, 1)
+    got(wdn.at[:, :, x], wdl_s)
+    d_own(0, 0)
+    g_relay(1, 1)
     g_relayed(0)
 
     @pl.loop(0, NX)
     def _(xs):
         hidden_of(0, xs)
 
-    def second_expert():
-        @pl.loop(0, NX - 1)
-        def _(step):
-            hidden_of(1, wrap(x + 3 + step, NX))
-
-        d_relay(early)
-        d_own(early + 1)
-        d_own(early + 2)
-        g_relayed(1)
-        hidden_of(1, opposite)
-
-    def down(u):
-        k, j = unit(u)
-        got(wdn.at[k, j, opposite], d_rs.at[u, 1])
+    @pl.loop(0, NX - 1)
+    def _(step):
+        hidden_of(1, wrap(x + 3 + step, NX))
+
+    d_relay(0, 0)
+    d_own(0, 1)
+    d_own(1, 0)
+    g_relayed(1)
+    hidden_of(1, opposite)
+
+    def down(k, j):
+        got(wdn.at[k, j, opposite], d_rs.at[k, j, 1])
         total = None
         for xs in range(NX):
             t = jnp.dot(hid[j, xs], wdn[k, j, xs], preferred_element_type=F32)
             total = t if total is None else total + t
         sb[k, :, j] = total.astype(BF16).reshape(NS, SLOTS, width)
         cb[k, mine, j] = sb[k, mine, j]
-        y_send(
-            lambda d: sb.at[k, d, j], lambda d: cb.at[k, d, j], lambda d: rl2.at[k, d, j],
-            y2_ss, y2_rs.at[k, j], l2_rs.at[k, j],
-        )
-
-    def pass_back(u):
-        k, j = unit(u)
-        y_forward(
-            lambda d: cb.at[k, d, j], lambda d: rl2.at[k, d, j], rl2.at[k, :, j],
-            f2_ss, y2_rs.at[k, j], l2_rs.at[k, j],
-        )
-
-    def r_hop(k, h):
-        s = 1 - 2 * lax.rem(k, 2)
+        for q in range(PARTS):
+            y_far(
+                lambda d: sb.at[k, d, j, :, part(q)], lambda d: rl2.at[k, d, j, :, part(q)],
+                y2_ss, l2_rs.at[k, j],
+            )
+        for q in range(PARTS):
+            y_send(
+                lambda d: sb.at[k, d, j, :, part(q)], lambda d: cb.at[k, d, j, :, part(q)],
+                y2_ss, y2_rs.at[k, q],
+            )
+
+    def part(q):
+        return pl.ds(q * thin, thin)
+
+    def pass_back(k, j):
+        got(rl2.at[k, :, j], l2_rs.at[k, j])
+        for q in range(PARTS):
+            y_forward(
+                lambda d: cb.at[k, d, j, :, part(q)], lambda d: rl2.at[k, d, j, :, part(q)],
+                f2_ss, y2_rs.at[k, q],
+            )
+
+    along = [wrap(z + o, NZ) for o in range(NZ)]
+
+    def r_hop(k, q, h):
+        s = 1 - 2 * q
+        cols = part(q)
         if h >= 2:
-            got(rsb.at[k, :, h - 2], r_rs.at[k, h - 2])
-        for way, t, step in ((0, z + (5 - h) * s, s), (1, z - (4 - h) * s, -s)):
+            got(rsb.at[k, :, h - 2, :, cols], r_rs.at[k, q, h - 2])
+        for way, t, step in ((0, (5 - h) * s, s), (1, (h - 4) * s, -s)):
             if h == 4 and way == 1:
                 continue
-            t = wrap(t, NZ)
+            t = along[t % NZ]
             if h >= 2:
-                xb[k, t] = (xb[k, t].astype(F32) + rsb[k, way, h - 2].astype(F32)).astype(BF16)
-            to = (x, y, wrap(z + step, NZ), c)
-            rcopy(xb.at[k, t], rsb.at[k, way, h - 1], r_ss, r_rs.at[k, h - 1], to).start()
-
-    def combine(k):
-        for j in range(PER):
-            got(cb.at[k, pl.ds(0, NS - 1), j], y2_rs.at[k, j])
-
-        @pl.loop(0, 2)
-        def _(p):
-            part = pl.ds(p * (NZ // 2), NZ // 2)
-            served = cb[k].reshape(NS * PER * SLOTS, width)
-            hi = wh[part].reshape(NZ // 2 * tok, NS * PER * SLOTS)
-            lo = wl[part].reshape(NZ // 2 * tok, NS * PER * SLOTS)
-            summed = jnp.dot(hi, served, preferred_element_type=F32)
-            summed += jnp.dot(lo, served, preferred_element_type=F32)
-            xb[k, part] = summed.astype(BF16).reshape(NZ // 2, tok, width)
-
-        r_hop(k, 1)
-
-    def out_copy(k):
-        return pltpu.make_async_copy(outb.at[k], out_ref.at[:, columns(k)], out_s)
-
-    def finish(k):
-        got(rsb.at[k, 0, 3], r_rs.at[k, 3])
-        value = xb[k, z].astype(F32) + rsb[k, 0, 3].astype(F32) + rsb[k, 1, 2].astype(F32)
-        outb[k] = value.astype(BF16)
-        out_copy(k).start()
-
-    def completed(u, fn):
-        k, j = unit(u)
-
-        @pl.when(jnp.logical_and(jnp.logical_and(u >= early, u < units), j == 1))
-        def _():
-            fn(k)
-
-    @pl.loop(0, units + 12)
+                held = xb[k, t, :, cols].astype(F32) + rsb[k, way, h - 2, :, cols].astype(F32)
+                xb[k, t, :, cols] = held.astype(BF16)
+            to = (x, y, along[step % NZ], c)
+            rcopy(
+                xb.at[k, t, :, cols], rsb.at[k, way, h - 1, :, cols], r_ss, r_rs.at[k, q, h - 1], to
+            ).start()
+
+    def combine(k, q):
+        got(cb.at[k, pl.ds(0, NS - 1), :, :, part(q)], y2_rs.at[k, q])
+        for pair in range(NZ // 2):
+            served = cb[k, :, :, 16 * pair : 16 * pair + SPAN, part(q)].reshape(NS * PER * SPAN, thin)
+            rows = ws[pair].reshape(4 * tok, NS * PER * SPAN)
+            summed = jnp.dot(rows, served, preferred_element_type=F32)
+            summed = summed[: 2 * tok] + summed[2 * tok :]
+            xb[k, 2 * pair : 2 * pair + 2, :, part(q)] = summed.astype(BF16).reshape(2, tok, thin)
+        r_hop(k, q, 1)
+
+    def out_copy(k, q):
+        at = pl.ds(pl.multiple_of(k * width + q * thin, thin), thin)
+        return pltpu.make_async_copy(outb.at[k, :, part(q)], out_ref.at[:, at], out_s)
+
+    def finish(k, q):
+        cols = part(q)
+        got(rsb.at[k, 0, 3, :, cols], r_rs.at[k, q, 3])
+        value = xb[k, z, :, cols].astype(F32) + rsb[k, 0, 3, :, cols].astype(F32)
+        value += rsb[k, 1, 2, :, cols].astype(F32)
+        outb[k, :, cols] = value.astype(BF16)
+        out_copy(k, q).start()
+
+    @pl.loop(0, NC + 5)
     def _(i):
-        guarded(i - 2, pass_back, 0, units)
-        completed(i - 12, finish)
-        completed(i - 10, lambda k: r_hop(k, 4))
-        completed(i - 8, lambda k: r_hop(k, 3))
-        completed(i - 6, lambda k: r_hop(k, 2))
-        completed(i - 4, combine)
-
-        @pl.when(i == early - 1)
-        def _():
-            d_own(early)
-            g_relay(1, 1)
-
-        @pl.when(i == early)
-        def _():
-            second_expert()
-
-        guarded(i + 1, d_relay, early + 1, units)
-        guarded(i + 3, d_own, early + 3, units)
-        guarded(i, down, 0, units)
-
-        @pl.when(i == early + 2)
+        guarded(i - 1, lambda k: pass_back(k, 0))
+        guarded(i - 3, lambda k: r_hop(k, 0, 2))
+        guarded(i - 4, lambda k: r_hop(k, 1, 3))
+        guarded(i, lambda k: d_relay(k, 1))
+        guarded(i + 1, lambda k: d_own(k, 1), 1)
+        guarded(i, lambda k: down(k, 0))
+        guarded(i - 2, lambda k: combine(k, 0))
+        guarded(i - 5, lambda k: finish(k, 0))
+        guarded(i - 3, lambda k: r_hop(k, 1, 2))
+
+        guarded(i - 1, lambda k: pass_back(k, 1))
+        guarded(i - 2, lambda k: combine(k, 1))
+        guarded(i - 4, lambda k: r_hop(k, 0, 4))
+        guarded(i - 5, lambda k: finish(k, 1))
+        guarded(i + 1, lambda k: d_relay(k, 0), 1)
+        guarded(i + 2, lambda k: d_own(k, 0), 2)
+        guarded(i, lambda k: down(k, 1))
+        guarded(i - 3, lambda k: r_hop(k, 0, 3))
+        guarded(i - 4, lambda k: r_hop(k, 1, 4))
+
+        @pl.when(i == 2)
         def _():
             c_step(4)
 
-        @pl.when(i == units - 2)
+        @pl.when(i == NC - 1)
         def _():
             c_step(5)
 
@@ -501,8 +494,7 @@
         scratch_shapes=[
             pltpu.VMEM((NC, NZ, tok, width), BF16),
             pltpu.VMEM((rows, NZ * tok), BF16),
-            pltpu.VMEM((NZ, tok, rows), BF16),
-            pltpu.VMEM((NZ, tok, rows), BF16),
+            pltpu.VMEM((NZ // 2, 2, 2, tok, NS * PER * SPAN), BF16),
             pltpu.VMEM((NC, NS, PER, SLOTS, width), BF16),
             pltpu.VMEM((NC, NS, PER, SLOTS, width), BF16),
             pltpu.VMEM((NC, NS, PER, SLOTS, width), BF16),
@@ -534,15 +526,15 @@
             dma((NC,)),
             dma,
             dma,
+            dma((NC, PARTS)),
             dma((NC, PER)),
-            dma((NC, PER)),
-            dma,
-            dma,
-            dma((NC, 4)),
+            dma,
+            dma,
+            dma((NC, PARTS, 4)),
             dma,
             dma((2, PER, 2)),
             dma,
-            dma((2 * NC, 2)),
+            dma((NC, PER, 2)),
         ],
         compiler_params=pltpu.CompilerParams(
             collective_id=0, has_side_effects=True, vmem_limit_bytes=67_043_328

time: 204 us -> 200 us (0.980)
  Pallas kernels: 202 us -> 199 us
    pallas_call x1, Pallas kernels: 201 us -> 197 us  [body(): pl.pallas_call(kernel, out_shape=(jax.ShapeDtypeStruct((tok, feat), BF16)...]
where the time goes in v3:
time: 200 us; the launch traced here: 199 us
  Pallas kernels  199 us (100%)
    pallas_call x1, Pallas kernels, body(): pl.pallas_call(kernel, out_shape=(jax.ShapeDtypeStruct((tok, feat), BF16)...  197 us

profile of v3, /device:TPU:8, one launch (start us, length us, event | category | flops | bytes accessed | tf_op | source)
XLA Modules:
  0.0 199.2 jit_solution(17227226711632880764)
XLA Ops:
  0.6 196.7 %moe_layer.1 = (bf16[128,2048]{1,0:T(8,128)(2,1)}, f32[1,128]{1,0:T(1,128)}) custom-call(s32[8,128]{1,0:T(8,128)} %bitcast.5, f32[8,128]{1,0:T(8,128)} %bitcast.6, bf16[128,2048]{1,0:T(8,128)(2,1)} %tok_ref.1, bf16[2,192,2048]{2,1,0:T(8,128)(2,1)} %wg_ref.1, bf16[2,192,2048]{2,1,0:T(8,128)(2,1)} %wu_ref.1, bf16[2,192,2048]{2,1,0:T(8,128)(2,1)} %wd_ref.1), custom_call_target="tpu_custom_call" | custom-call | tf_op jit(solution)/shard_map/moe_layer/pallas_call | solution.py:486
  197.4 1.9 moe_close.1

commit v4 on v3

--- a/solution.py
+++ b/solution.py
@@ -33,8 +33,8 @@
 def kernel(
     route_ref, weight_ref, tok_ref, wg_ref, wu_ref, wd_ref,
     out_ref, cnt_ref,
-    xb, pm, ws, sb, rb, cb, wgu, wdn, hid, rl1, rl2, rsb, mroute, mweight, keys, wks, csend, crecv, outb,
-    loc_s, tok_s, wdl_s, out_s, meta_ss, meta_rs, c_ss, c_rs,
+    xb, pm, ws, sb, rb, cb, wgu, wdn, hid, rl1, rl2, rsb, mroute, mweight, keys, wks, csend, crecv, ctotal, outb,
+    loc_s, tok_s, wdl_s, out_s, tot_s, meta_ss, meta_rs, c_ss, c_rs,
     z_ss, z_rs, y1_ss, y1_rs, l1_rs, f1_ss, y2_ss, y2_rs, l2_rs, f2_ss, r_ss, r_rs,
     g_ss, g_rs, d_ss, d_rs,
 ):
@@ -66,6 +66,12 @@
         pltpu.make_async_copy(wg_ref, wgu.at[0, :, x], loc_s.at[0]),
         pltpu.make_async_copy(wu_ref, wgu.at[1, :, x], loc_s.at[1]),
     ]
+    own_m = [
+        pltpu.make_async_copy(route_ref, mroute.at[z], loc_s.at[2]),
+        pltpu.make_async_copy(weight_ref, mweight.at[z], loc_s.at[3]),
+    ]
+    own_m[0].start()
+    own_m[1].start()
     own_g[0].start()
     own_g[1].start()
 
@@ -132,23 +138,23 @@
             rcopy(near, near, z_ss, z_rs.at[k, h - 1], (x, y, wrap(z - s, NZ), c)).start()
 
     def m_hop(h):
-        for a, (own, held) in enumerate(((route_ref, mroute), (weight_ref, mweight))):
+        for a, held in enumerate((mroute, mweight)):
             if h >= 2:
                 got(held.at[pl.ds(0, 2)], meta_rs.at[a, h - 2])
             p, q = wrap(z - (h - 1), NZ), wrap(z + (h - 1), NZ)
             rcopy(
-                own if h == 1 else held.at[p], held.at[p], meta_ss.at[a], meta_rs.at[a, h - 1],
+                held.at[p], held.at[p], meta_ss.at[a], meta_rs.at[a, h - 1],
                 (x, y, wrap(z + 1, NZ), c),
             ).start()
             if h < 4:
                 rcopy(
-                    own if h == 1 else held.at[q], held.at[q], meta_ss.at[a], meta_rs.at[a, h - 1],
+                    held.at[q], held.at[q], meta_ss.at[a], meta_rs.at[a, h - 1],
                     (x, y, wrap(z - 1, NZ), c),
                 ).start()
 
+    own_m[0].wait()
+    own_m[1].wait()
     m_hop(1)
-    mroute[z] = route_ref[...]
-    mweight[z] = weight_ref[...]
     tok_copy(0).wait()
     z_hop(0, 1)
     m_hop(2)
@@ -255,7 +261,7 @@
             c_move(s - 1).wait()
             total = csend[s - 1] + crecv[s - 1]
         if s == len(partners):
-            cnt_ref[...] = total[0:1]
+            ctotal[...] = total
             return
         if s > 0:
             csend[s] = total
@@ -428,6 +434,8 @@
         outb[k, :, cols] = value.astype(BF16)
         out_copy(k, q).start()
 
+    total_copy = pltpu.make_async_copy(ctotal, cnt_ref, tot_s)
+
     @pl.loop(0, NC + 5)
     def _(i):
         guarded(i - 1, lambda k: pass_back(k, 0))
@@ -458,17 +466,22 @@
         def _():
             c_step(5)
 
+        @pl.when(i == NC + 1)
+        def _():
+            total_copy.start()
+
     sent(wgu.at[:, :, pl.ds(0, NX - 1)], g_ss)
     sent(wdn.at[:, :, pl.ds(0, NX - 1)], d_ss)
     sent(sb.at[:, pl.ds(0, NS - 1)], y2_ss)
     sent(rl2, f2_ss)
     sent(xb.at[:, pl.ds(0, NZ - 1)], r_ss)
     got(outb, out_s)
+    total_copy.wait()
 
 
 def close(mean_load, experts, mixed_ref, total_ref, bias_ref, out_ref, new_bias_ref, count_ref):
     out_ref[...] = mixed_ref[...]
-    totals = total_ref[...]
+    totals = total_ref[0:1]
     over = mean_load - experts * totals
     sign = jnp.where(over > 0.0, 1.0, jnp.where(over < 0.0, -1.0, 0.0))
     new_bias_ref[...] = bias_ref[...] + bias_rate * sign
@@ -487,10 +500,10 @@
         kernel,
         out_shape=(
             jax.ShapeDtypeStruct((tok, feat), BF16),
-            jax.ShapeDtypeStruct((1, experts), F32),
+            jax.ShapeDtypeStruct((8, experts), F32),
         ),
-        in_specs=[vmem, vmem, anywhere, anywhere, anywhere, anywhere],
-        out_specs=(anywhere, vmem),
+        in_specs=[anywhere, anywhere, anywhere, anywhere, anywhere, anywhere],
+        out_specs=(anywhere, anywhere),
         scratch_shapes=[
             pltpu.VMEM((NC, NZ, tok, width), BF16),
             pltpu.VMEM((rows, NZ * tok), BF16),
@@ -510,9 +523,11 @@
             pltpu.VMEM((NZ, NS * PER, tok), F32),
             pltpu.VMEM((5, 8, tok), F32),
             pltpu.VMEM((5, 8, tok), F32),
+            pltpu.VMEM((8, tok), F32),
             pltpu.VMEM((NC, tok, width), BF16),
+            dma((4,)),
             dma((2,)),
-            dma((2,)),
+            dma,
             dma,
             dma,
             dma((2,)),

time: 200 us -> 198 us (0.990)
  no operation moved by 1% of the time
where the time goes in v4:
time: 198 us
  Pallas kernels  198 us (100%)
    pallas_call x1, Pallas kernels, body(): pl.pallas_call(kernel, out_shape=(jax.ShapeDtypeStruct((tok, feat), BF16)...  196 us

profile of v4, /device:TPU:8, one launch (start us, length us, event | category | flops | bytes accessed | tf_op | source)
XLA Modules:
  0.0 198.3 jit_solution(1273207449802089588)
XLA Ops:
  0.6 195.8 %moe_layer.1 = (bf16[128,2048]{1,0:T(8,128)(2,1)}, f32[8,128]{1,0:T(8,128)}) custom-call(s32[8,128]{1,0:T(8,128)} %bitcast.5, f32[8,128]{1,0:T(8,128)} %bitcast.6, bf16[128,2048]{1,0:T(8,128)(2,1)} %tok_ref.1, bf16[2,192,2048]{2,1,0:T(8,128)(2,1)} %wg_ref.1, bf16[2,192,2048]{2,1,0:T(8,128)(2,1)} %wu_ref.1, bf16[2,192,2048]{2,1,0:T(8,128)(2,1)} %wd_ref.1), custom_call_target="tpu_custom_call" | custom-call | tf_op jit(solution)/shard_map/moe_layer/pallas_call | solution.py:499
  196.4 1.9 moe_close.1
